TPU v7x, 256 devices: a whole 4x4x8 slice. The times are simulated.
256 devices in a mesh: prow: 16 (over y_hi, z), pcol: 16 (over x, y_lo, core).
Axes of the slice: x: 4, y: 4 (y_hi: 2, y_lo: 2; y = y_hi * 2 + y_lo), z: 8, core: 2. Of those that a mesh axis runs over, the one named last changes fastest.
Arguments:
- a_panel: float32 [98304, 512], P('prow', 'pcol'), may hold values from -6 to 6
- u_rows: float32 [512, 98304], P('pcol', 'prow'), may hold values from -0.25 to 0.25
- u_col: float32 [98304, 2048], P('prow', 'pcol'), may hold values from -0.01953125 to 0.01953125
- c_in: float32 [98304, 2048], P('prow', 'pcol'), may hold values from -6 to 6
Outputs:
- c_out: float32 [98304, 2048], P('prow', 'pcol')
All inputs are finite; a program needn't handle non-finite values.
Results may differ from a plain program's by a relative error of at most 0.00007.
Values sent between devices are 32-bit elements; how exact they have to be, the bound alone decides.
No kernel may reach another device: no remote copies, remote signals or barrier semaphores. Data moves between devices by JAX's collectives and lax.ppermute only.
A program may use at most 128 MiB of HBM per device.

v0:
```python
import jax
import jax.numpy as jnp
from jax import lax
from jax.sharding import PartitionSpec as P


def cut_along(x, dim, devices):
    before, after = (x.shape[:dim], x.shape[dim + 1 :])
    return jnp.moveaxis(x.reshape(*before, devices, -1, *after), dim, 0)


def summed_on_arrival(x, axis, dim):
    devices = lax.axis_size(axis)
    tiles = lax.all_to_all(cut_along(x, dim, devices), axis, 0, 0, tiled=True)
    return jnp.sum(tiles, axis=0)


def laid_out(tiles, dim):
    tiles = jnp.moveaxis(tiles, 0, dim)
    lengths = tiles.shape
    return tiles.reshape(*lengths[:dim], lengths[dim] * lengths[dim + 1], *lengths[dim + 2 :])


def sent_to_all(x, axis):
    copies = jnp.broadcast_to(x, (lax.axis_size(axis), *x.shape))
    return lax.all_to_all(copies, axis, split_axis=0, concat_axis=0, tiled=True)


def gather_directly(x, axis, dim):
    return laid_out(sent_to_all(x, axis), dim)


def on_device(a_panel, u_rows, u_col, c_in):
    a_full, u_full = (
        lax.all_gather(a_panel, "pcol", axis=1, tiled=True),
        lax.all_gather(u_rows, "pcol", axis=0, tiled=True),
    )
    inner_share = summed_on_arrival(
        jnp.dot(
            a_full.T, u_col, precision=lax.Precision.HIGHEST, preferred_element_type=jnp.float32
        ),
        "prow",
        0,
    )
    return c_in + jnp.dot(
        u_full.T,
        gather_directly(inner_share, "prow", 0),
        precision=lax.Precision.HIGHEST,
        preferred_element_type=jnp.float32,
    )


def solution(mesh):
    placed = (P("prow", "pcol"), P("pcol", "prow"), P("prow", "pcol"), P("prow", "pcol"))
    return jax.shard_map(
        on_device, mesh=mesh, in_specs=placed, out_specs=P("prow", "pcol"), check_vma=False
    )
```

profile of v0, /device:TPU:1, one launch (start us, length us, event | category | flops | bytes accessed | tf_op | source)
XLA Modules:
  0.0 193.7 jit_solution(4302002737189575478)
XLA Ops:
  6.5 0.0 copy-start
  6.5 0.0 all-gather.3.cloned.1.call-start
  6.5 0.7 all-gather.3.cloned.1.call-update
  7.3 0.0 all-gather.5.cloned.1.call-start
  7.3 0.7 all-gather.5.cloned.1.call-update
  8.0 79.7 %all-gather.3.cloned.1.call-done = f32[6144,512]{0,1:T(8,128)} async-done(((f32[6144,32]{0,1:T(8,128)}), f32[6144,512]{0,1:T(8,128)}) %all-gather.3.cloned.1.call-update) | async-done | bytes 12582928 | tf_op jit(solution)/shard_map/all_gather | solution.py:35
  87.8 0.0 copy-done
  87.8 12.5 %fusion.1 = f32[512,128]{1,0:T(8,128)S(1)} fusion(f32[6144,512]{0,1:T(8,128)} %all-gather.3.cloned.1.call-done, f32[6144,128]{1,0:T(8,128)S(1)} %copy-done), kind=kOutput, calls=%fused_computation.2 | convolution fusion | flops 4831838208 | bytes 15990784 | tf_op jit(solution)/shard_map/dot_general | solution.py:39
  100.2 19.5 %all_to_all.10 = f32[16,32,128]{2,1,0:T(8,128)S(1)} all-to-all(f32[16,32,128]{2,1,0:T(8,128)S(1)} %bitcast.11), channel_id=1, replica_groups=mesh['prow'=16,'pcol'=16] {'prow'}, dimensions={0} | all-to-all | bytes 524288 | tf_op jit(solution)/shard_map/all_to_all | solution.py:14
  119.7 0.7 broadcast_in_dim.3
  120.5 5.4 %all-to-all-start.1 = ((f32[16,32,128]{2,1,0:T(8,128)}), f32[16,32,128]{2,1,0:T(8,128)S(1)}, u32[]{:S(2)}, u32[]{:S(2)}) async-start(f32[16,32,128]{2,1,0:T(8,128)} %broadcast_in_dim.3), calls=%async_computation.1 | async-start | bytes 524288 | tf_op jit(solution)/shard_map/all_to_all | solution.py:26
  125.9 3.6 %copy.5 = f32[6144,128]{0,1:T(8,128)} copy(f32[6144,128]{1,0:T(8,128)} %param.7) | data formatting | bytes 6291456 | tf_op args[3]
  129.5 41.0 %all-gather.5.cloned.1.call-done = f32[512,6144]{1,0:T(8,128)} async-done(((f32[32,6144]{1,0:T(8,128)}), f32[512,6144]{1,0:T(8,128)}) %all-gather.5.cloned.1.call-update) | async-done | bytes 12582928 | tf_op jit(solution)/shard_map/all_gather | solution.py:36
  170.4 0.0 all-to-all-done.1
  170.5 12.9 %fusion = f32[6144,128]{0,1:T(8,128)} fusion(f32[6144,128]{0,1:T(8,128)} %copy.5, f32[512,128]{1,0:T(8,128)S(1)} %bitcast.10, f32[512,6144]{1,0:T(8,128)} %all-gather.5.cloned.1.call-done), kind=kOutput, calls=%fused_computation.1 | convolution fusion | flops 4832624640 | bytes 19136512 | tf_op jit(solution)/shard_map/dot_general | solution.py:45
  183.3 3.5 %copy.6 = f32[6144,128]{1,0:T(8,128)} copy(f32[6144,128]{0,1:T(8,128)} %fusion) | data formatting | bytes 6291456 | tf_op jit(solution)/shard_map/add | solution.py:45
  (1 shorter events, 0.0 us)
Async XLA Ops:
  6.5 81.2 %copy-start = (f32[6144,128]{1,0:T(8,128)S(1)}, f32[6144,128]{1,0:T(8,128)}, u32[]{:S(2)}) copy-start(f32[6144,128]{1,0:T(8,128)} %param.6) | copy-start | bytes 9437188
  6.5 81.2 %all-gather.3.cloned.1.call-start = ((), (), s32[]{:S(2)}) async-start(), calls=%async_computation.2 | async-start | bytes 13369344 | tf_op jit(solution)/shard_map/all_gather | solution.py:35
  7.3 163.2 %all-gather.5.cloned.1.call-start = ((), (), s32[]{:S(2)}) async-start(), calls=%async_computation.3 | async-start | bytes 13369344 | tf_op jit(solution)/shard_map/all_gather | solution.py:36
  120.5 50.0 %all-to-all-start.1 = ((f32[16,32,128]{2,1,0:T(8,128)}), f32[16,32,128]{2,1,0:T(8,128)S(1)}, u32[]{:S(2)}, u32[]{:S(2)}) async-start(f32[16,32,128]{2,1,0:T(8,128)} %broadcast_in_dim.3), calls=%async_computation.1 | async-start | bytes 524288 | tf_op jit(solution)/shard_map/all_to_all | solution.py:26
Sparse Core Ops, SparseCore 0:
  9.2 78.5 all-gather.2
  89.6 80.8 all-gather.4
where the time goes:
time: 194 us
  waiting for transfers between devices  122 us (63%)
  matrix products  25.3 us (13%)
  blocking collectives  19.5 us (10%)
  between operations  13.4 us (7%)
  local copies, waits for them, and re-layouts  7.86 us (4%)
  starting transfers between devices  5.45 us (3%)
    all_gather x1, waiting for transfers between devices, on_device(): lax.all_gather(a_panel, 'pcol', axis=1, tiled=True)  79.7 us
    all_gather x1, waiting for transfers between devices, on_device(): lax.all_gather(u_rows, 'pcol', axis=0, tiled=True)  41 us
    all_to_all x1, blocking collectives, summed_on_arrival(): tiles = lax.all_to_all(cut_along(x, dim, devices), axis, 0, 0, tiled=True)  19.5 us
    dot_general x1, matrix products, on_device(): jnp.dot(u_full.T, gather_directly(inner_share, 'prow', 0), precision=lax....  12.9 us
    dot_general x1, matrix products, on_device(): jnp.dot(a_full.T, u_col, precision=lax.Precision.HIGHEST, preferred_eleme...  12.5 us
    all_to_all x1, starting transfers between devices, sent_to_all(): return lax.all_to_all(copies, axis, split_axis=0, concat_axis=0, tiled=True)  5.41 us
  transfers between devices with their start and end apart: 3, of which 2 were waited for; matrix products, arithmetic and copies ran while one was open for 9% of the time, Pallas kernels for 0%

commit v1 on v0

v1 whole, which is shorter than its diff:
```python
import jax
import jax.numpy as jnp
from jax import lax
from jax.sharding import PartitionSpec as P

ROUTES = (
    (0, "+", "+"),
    (0, "y", "-"),
    (0, "-", "y"),
    (2, "+", "y"),
    (2, "-", "-"),
    (1, "+", "y"),
    (5, "-", "y"),
)
C_CHUNKS = 2


def target(at, move):
    x, y, core = at // 4, at // 2 % 2, at % 2
    if move == "y":
        y = 1 - y
    else:
        x = (x + (1 if move == "+" else -1)) % 4
    return (x * 2 + y) * 2 + core


def pairs(moves):
    return [(at, target(at, moves[at % 2])) for at in range(16)]


def gather_blocks(own):
    held = [own]
    for source, *moves in ROUTES:
        held.append(lax.ppermute(held[source], "pcol", pairs(moves)))
    return held


def placed_blocks(blocks):
    k, n = blocks[0].shape
    out = jnp.zeros((k * len(blocks), n), blocks[0].dtype)
    for i, block in enumerate(blocks):
        out = lax.dynamic_update_slice(out, block, (i * k, 0))
    return out


def swapped(x):
    return lax.ppermute(x, "pcol", [(at, at ^ 1) for at in range(16)])


def product(a, b):
    return jnp.dot(a, b, precision=lax.Precision.HIGH, preferred_element_type=jnp.float32)


def on_device(a_panel, u_rows, u_col, c_in):
    other_col = swapped(u_col)
    a = jnp.concatenate(gather_blocks(a_panel.T), axis=0)
    u = gather_blocks(u_rows)
    partial = product(a, jnp.concatenate([u_col, other_col], axis=1))
    tiles = partial.reshape(16, partial.shape[0] // 16, partial.shape[1])
    tiles = lax.all_to_all(tiles, "prow", 0, 0, tiled=True)
    share = jnp.sum(tiles, axis=0)
    copies = jnp.broadcast_to(share, tiles.shape)
    inner = lax.all_to_all(copies, "prow", 0, 0, tiled=True).reshape(partial.shape)
    u = placed_blocks(u)
    rows, width = c_in.shape[0] // C_CHUNKS, c_in.shape[1]
    done = []
    for i in range(C_CHUNKS):
        c = product(u[:, i * rows : (i + 1) * rows].T, inner)
        other = swapped(c[:, width:])
        done.append(c_in[i * rows : (i + 1) * rows] + c[:, :width] + other)
    return jnp.concatenate(done, axis=0)


def solution(mesh):
    placed = (P("prow", "pcol"), P("pcol", "prow"), P("prow", "pcol"), P("prow", "pcol"))
    return jax.shard_map(
        on_device, mesh=mesh, in_specs=placed, out_specs=P("prow", "pcol"), check_vma=False
    )
```

time: 194 us -> 145 us (0.75)
  waiting for transfers between devices: 122 us -> 79.2 us
  starting transfers between devices: 5.45 us -> 36.1 us
  blocking collectives: 19.5 us -> 0 us
  between operations: 13.4 us -> 0.16 us
  matrix products: 25.3 us -> 13.2 us
  local copies, waits for them, and re-layouts: 7.86 us -> 13.6 us
  other arithmetic: 0.02 us -> 2.31 us
    all_gather x2 -> x0, waiting for transfers between devices: 121 us -> none  [the longest x1 79.7 us: on_device(): lax.all_gather(a_panel, 'pcol', axis=1, tiled=True)]
    ppermute x0 -> x17, waiting for transfers between devices: none -> 62.6 us  [the longest x14 57.5 us: gather_blocks(): held.append(lax.ppermute(held[source], 'pcol', pairs(moves)))]
    ppermute x0 -> x17, starting transfers between devices: none -> 22.5 us  [the longest x14 12 us: gather_blocks(): held.append(lax.ppermute(held[source], 'pcol', pairs(moves)))]
    all_to_all x1 -> x0, blocking collectives: 19.5 us -> none  [summed_on_arrival(): tiles = lax.all_to_all(cut_along(x, dim, devices), axis, 0, 0, tiled=True)]
    all_to_all x1 -> x2, waiting for transfers between devices: 0.01 us -> 16.6 us  [the longest x1 8.32 us: on_device(): lax.all_to_all(copies, 'prow', 0, 0, tiled=True).reshape(partial.shape)]
    dot_general x2 -> x3, matrix products: 25.3 us -> 13.2 us  [product(): jnp.dot(a, b, precision=lax.Precision.HIGH, preferred_element_type=jnp.fl...]
    dynamic_update_slice x0 -> x8, local copies, waits for them, and re-layouts: none -> 11.1 us  [placed_blocks(): out = lax.dynamic_update_slice(out, block, (i * k, 0))]
    all_to_all x1 -> x2, starting transfers between devices: 5.41 us -> 13.6 us  [the longest x1 9.57 us: on_device(): tiles = lax.all_to_all(tiles, 'prow', 0, 0, tiled=True)]
  transfers between devices with their start and end apart: 3 -> 19, of which waited for: 2 -> 11; matrix products, arithmetic and copies ran while one was open for 9% -> 12% of each run, Pallas kernels for 0% -> 0%
where the time goes in v1:
time: 145 us
  waiting for transfers between devices  79.2 us (55%)
  starting transfers between devices  36.1 us (25%)
  local copies, waits for them, and re-layouts  13.6 us (9%)
  matrix products  13.2 us (9%)
  other arithmetic  2.31 us (2%)
    ppermute x14, waiting for transfers between devices, gather_blocks(): held.append(lax.ppermute(held[source], 'pcol', pairs(moves)))  57.5 us
    dot_general x3, matrix products, product(): jnp.dot(a, b, precision=lax.Precision.HIGH, preferred_element_type=jnp.fl...  13.2 us
    ppermute x14, starting transfers between devices, gather_blocks(): held.append(lax.ppermute(held[source], 'pcol', pairs(moves)))  12 us
    dynamic_update_slice x8, local copies, waits for them, and re-layouts, placed_blocks(): out = lax.dynamic_update_slice(out, block, (i * k, 0))  11.1 us
    ppermute x3, starting transfers between devices, swapped(): return lax.ppermute(x, 'pcol', [(at, at ^ 1) for at in range(16)])  10.5 us
    all_to_all x1, starting transfers between devices, on_device(): tiles = lax.all_to_all(tiles, 'prow', 0, 0, tiled=True)  9.57 us
    all_to_all x1, waiting for transfers between devices, on_device(): lax.all_to_all(copies, 'prow', 0, 0, tiled=True).reshape(partial.shape)  8.32 us
    all_to_all x1, waiting for transfers between devices, on_device(): tiles = lax.all_to_all(tiles, 'prow', 0, 0, tiled=True)  8.3 us
  transfers between devices with their start and end apart: 19, of which 11 were waited for; matrix products, arithmetic and copies ran while one was open for 12% of the time, Pallas kernels for 0%

profile of v1, /device:TPU:1, one launch (start us, length us, event | category | flops | bytes accessed | tf_op | source)
XLA Modules:
  0.0 144.6 jit_solution(55475169321045256)
XLA Ops:
  0.0 3.3 %collective-permute-start.8 = (f32[32,6144]{1,0:T(8,128)}, f32[32,6144]{1,0:T(8,128)S(1)}, u32[]{:S(2)}, u32[]{:S(2)}) collective-permute-start(f32[32,6144]{1,0:T(8,128)} %bitcast.9), channel_id=1, source_target_pairs={{0,2},{1,13},{2,0},{3,15},{4,6},{5,1},{6,4},{7,3},{8,10},{9,5},{10... | collective-permute-start | bytes 2359304 | tf_op jit(solution)/shard_map/ppermute | solution.py:34
  3.3 1.3 collective-permute-start.9
  4.6 2.7 %collective-permute-start.1 = (f32[32,6144]{1,0:T(8,128)}, f32[32,6144]{1,0:T(8,128)S(1)}, u32[]{:S(2)}, u32[]{:S(2)}) collective-permute-start(f32[32,6144]{1,0:T(8,128)} %param.5), channel_id=1, source_target_pairs={{0,2},{1,13},{2,0},{3,15},{4,6},{5,1},{6,4},{7,3},{8,10},{9,5},{10... | collective-permute-start | bytes 2359304 | tf_op jit(solution)/shard_map/ppermute | solution.py:34
  7.3 1.2 constant_dynamic-update-slice_fusion.7
  8.5 4.5 %dynamic_update_slice.24 = f32[256,6144]{1,0:T(8,128)} pad(f32[32,6144]{1,0:T(8,128)} %param.5, f32[]{:T(128)} %constant.9.clone.1), padding=0_224x0_0 | pad | bytes 7077892 | tf_op jit(solution)/shard_map/dynamic_update_slice | solution.py:42
  12.9 11.0 %collective-permute-done.7 = f32[32,6144]{1,0:T(8,128)S(1)} collective-permute-done((f32[32,6144]{1,0:T(8,128)}, f32[32,6144]{1,0:T(8,128)S(1)}, u32[]{:S(2)}, u32[]{:S(2)}) %collective-permute-start.7) | collective-permute-done | bytes 786464 | tf_op jit(solution)/shard_map/ppermute | solution.py:34
  24.8 1.8 %collective-permute-start.14 = (f32[6144,128]{1,0:T(8,128)S(1)}, f32[6144,128]{1,0:T(8,128)S(1)}, u32[]{:S(2)}, u32[]{:S(2)}) collective-permute-start(f32[6144,128]{1,0:T(8,128)S(1)} %copy-done), channel_id=1, source_target_pairs={{0,1},{1,0},{2,3},{3,2},{4,5},{5,4},{6,7},{7,6},{8,9},{9,8},{10,11... | collective-permute-start | bytes 9437192 | tf_op jit(solution)/shard_map/ppermute | solution.py:47
  27.2 13.6 %collective-permute-done = f32[32,6144]{1,0:T(8,128)S(1)} collective-permute-done((f32[32,6144]{1,0:T(8,128)}, f32[32,6144]{1,0:T(8,128)S(1)}, u32[]{:S(2)}, u32[]{:S(2)}) %collective-permute-start) | collective-permute-done | bytes 786464 | tf_op jit(solution)/shard_map/ppermute | solution.py:34
  40.8 1.0 constant_dynamic-update-slice_fusion.14
  42.6 0.9 constant_dynamic-update-slice_fusion.13
  44.1 0.9 constant_dynamic-update-slice_fusion.12
  45.1 3.3 %collective-permute-done.10 = f32[32,6144]{1,0:T(8,128)S(1)} collective-permute-done((f32[32,6144]{1,0:T(8,128)S(1)}, f32[32,6144]{1,0:T(8,128)S(1)}, u32[]{:S(2)}, u32[]{:S(2)}) %collective-permute-start.10) | collective-permute-done | bytes 786464 | tf_op jit(solution)/shard_map/ppermute | solution.py:34
  48.4 1.1 collective-permute-start.4
  49.5 9.6 %collective-permute-done.11 = f32[32,6144]{1,0:T(8,128)S(1)} collective-permute-done((f32[32,6144]{1,0:T(8,128)S(1)}, f32[32,6144]{1,0:T(8,128)S(1)}, u32[]{:S(2)}, u32[]{:S(2)}) %collective-permute-start.11) | collective-permute-done | bytes 786464 | tf_op jit(solution)/shard_map/ppermute | solution.py:34
  59.6 5.6 %collective-permute-done.3 = f32[32,6144]{1,0:T(8,128)S(1)} collective-permute-done((f32[32,6144]{1,0:T(8,128)S(1)}, f32[32,6144]{1,0:T(8,128)S(1)}, u32[]{:S(2)}, u32[]{:S(2)}) %collective-permute-start.3) | collective-permute-done | bytes 786464 | tf_op jit(solution)/shard_map/ppermute | solution.py:34
  65.3 10.7 %collective-permute-done.4 = f32[32,6144]{1,0:T(8,128)S(1)} collective-permute-done((f32[32,6144]{1,0:T(8,128)S(1)}, f32[32,6144]{1,0:T(8,128)S(1)}, u32[]{:S(2)}, u32[]{:S(2)}) %collective-permute-start.4) | collective-permute-done | bytes 786464 | tf_op jit(solution)/shard_map/ppermute | solution.py:34
  76.4 1.0 constant_dynamic-update-slice_fusion.11
  77.3 0.9 constant_dynamic-update-slice_fusion.10
  78.3 3.8 %collective-permute-done.13 = f32[32,6144]{1,0:T(8,128)S(1)} collective-permute-done((f32[32,6144]{1,0:T(8,128)S(1)}, f32[32,6144]{1,0:T(8,128)S(1)}, u32[]{:S(2)}, u32[]{:S(2)}) %collective-permute-start.13) | collective-permute-done | bytes 786464 | tf_op jit(solution)/shard_map/ppermute | solution.py:34
  82.1 3.9 %fusion = f32[256,256]{1,0:T(8,128)} fusion(f32[256,6144]{1,0:T(8,128)S(1)} %constant_dynamic-update-slice_fusion, f32[6144,128]{1,0:T(8,128)S(1)} %collective-permute-done.14, f32[6144,128]{1,0:T(8,128)S(1)} %copy-done), kind=kOutput, calls=%fused_computation | convolution fusion | flops 2417491968 | bytes 12845056 | tf_op jit(solution)/shard_map/dot_general | solution.py:51
  86.0 9.6 %all-to-all-start = ((f32[16,16,256]{2,1,0:T(8,128)}), f32[16,16,256]{2,1,0:T(8,128)S(1)}, u32[]{:S(2)}, u32[]{:S(2)}) async-start(f32[16,16,256]{2,1,0:T(8,128)} %bitcast.1), calls=%async_computation | async-start | bytes 524288 | tf_op jit(solution)/shard_map/all_to_all | solution.py:60
  95.6 0.9 constant_dynamic-update-slice_fusion.9
  96.6 8.3 %all-to-all-done = f32[16,16,256]{2,1,0:T(8,128)S(1)} async-done(((f32[16,16,256]{2,1,0:T(8,128)}), f32[16,16,256]{2,1,0:T(8,128)S(1)}, u32[]{:S(2)}, u32[]{:S(2)}) %all-to-all-start) | async-done | bytes 262176 | tf_op jit(solution)/shard_map/all_to_all | solution.py:60
  105.6 4.0 %all-to-all-start.1 = ((f32[16,16,256]{2,1,0:T(8,128)}), f32[16,16,256]{2,1,0:T(8,128)S(1)}, u32[]{:S(2)}, u32[]{:S(2)}) async-start(f32[16,16,256]{2,1,0:T(8,128)} %broadcast_in_dim.4), calls=%async_computation.1 | async-start | bytes 524288 | tf_op jit(solution)/shard_map/all_to_all | solution.py:63
  109.7 0.9 constant_dynamic-update-slice_fusion.8
  110.6 8.3 %all-to-all-done.1 = f32[16,16,256]{2,1,0:T(8,128)S(1)} async-done(((f32[16,16,256]{2,1,0:T(8,128)}), f32[16,16,256]{2,1,0:T(8,128)S(1)}, u32[]{:S(2)}, u32[]{:S(2)}) %all-to-all-start.1) | async-done | bytes 262176 | tf_op jit(solution)/shard_map/all_to_all | solution.py:63
  119.0 4.6 %fusion.4 = f32[3072,256]{1,0:T(8,128)S(1)} fusion(f32[256,256]{1,0:T(8,128)S(1)} %bitcast.7, f32[256,6144]{1,0:T(8,128)} %constant_dynamic-update-slice_fusion.8), kind=kOutput, calls=%fused_computation.4 | convolution fusion | flops 1207959552 | bytes 6553600 | tf_op jit(solution)/shard_map/dot_general | solution.py:51
  123.6 4.7 %fusion.6 = f32[3072,256]{1,0:T(8,128)S(1)} fusion(f32[256,256]{1,0:T(8,128)S(1)} %bitcast.8, f32[256,6144]{1,0:T(8,128)} %constant_dynamic-update-slice_fusion.8), kind=kOutput, calls=%fused_computation.6 | convolution fusion | flops 1207959552 | bytes 6553600 | tf_op jit(solution)/shard_map/dot_general | solution.py:51
  128.4 8.6 %collective-permute-start.16 = (f32[3072,128]{1,0:T(8,128)S(1)}, f32[3072,128]{1,0:T(8,128)S(1)}, u32[]{:S(2)}, u32[]{:S(2)}) collective-permute-start(f32[3072,128]{1,0:T(8,128)S(1)} %slice.37), channel_id=1, source_target_pairs={{0,1},{1,0},{2,3},{3,2},{4,5},{5,4},{6,7},{7,6},{8,9},{9,8},{10,11... | collective-permute-start | bytes 4718600 | tf_op jit(solution)/shard_map/ppermute | solution.py:47
  137.2 2.8 %collective-permute-done.16 = f32[3072,128]{1,0:T(8,128)S(1)} collective-permute-done((f32[3072,128]{1,0:T(8,128)S(1)}, f32[3072,128]{1,0:T(8,128)S(1)}, u32[]{:S(2)}, u32[]{:S(2)}) %collective-permute-start.16) | collective-permute-done | bytes 1572896 | tf_op jit(solution)/shard_map/ppermute | solution.py:47
  140.0 2.2 %collective-permute-done.15 = f32[3072,128]{1,0:T(8,128)S(1)} collective-permute-done((f32[3072,128]{1,0:T(8,128)S(1)}, f32[3072,128]{1,0:T(8,128)S(1)}, u32[]{:S(2)}, u32[]{:S(2)}) %collective-permute-start.15) | collective-permute-done | bytes 1572896 | tf_op jit(solution)/shard_map/ppermute | solution.py:47
  142.7 1.9 %pad_maximum_fusion = f32[6144,128]{1,0:T(8,128)} fusion(f32[3072,128]{1,0:T(8,128)S(1)} %get-tuple-element.6, f32[3072,128]{1,0:T(8,128)S(1)} %get-tuple-element.5), kind=kLoop, calls=%fused_computation.8 | loop fusion | flops 786432 | bytes 6291456 | tf_op jit(solution)/shard_map/concatenate | solution.py:71
  (37 shorter events, 5.5 us)
Async XLA Ops:
  0.0 23.9 %copy-start.2 = (f32[32,6144]{1,0:T(8,128)S(1)}, f32[32,6144]{1,0:T(8,128)}, u32[]{:S(2)}) copy-start(f32[32,6144]{1,0:T(8,128)} %param.5) | copy-start | bytes 2359300
  0.0 24.8 %copy-start = (f32[6144,128]{1,0:T(8,128)S(1)}, f32[6144,128]{1,0:T(8,128)}, u32[]{:S(2)}) copy-start(f32[6144,128]{1,0:T(8,128)} %param.6) | copy-start | bytes 9437188
  0.0 24.8 %collective-permute-start.8 = (f32[32,6144]{1,0:T(8,128)}, f32[32,6144]{1,0:T(8,128)S(1)}, u32[]{:S(2)}, u32[]{:S(2)}) collective-permute-start(f32[32,6144]{1,0:T(8,128)} %bitcast.9), channel_id=1, source_target_pairs={{0,2},{1,13},{2,0},{3,15},{4,6},{5,1},{6,4},{7,3},{8,10},{9,5},{10... | collective-permute-start | bytes 2359304 | tf_op jit(solution)/shard_map/ppermute | solution.py:34
  3.3 20.6 %collective-permute-start.7 = (f32[32,6144]{1,0:T(8,128)}, f32[32,6144]{1,0:T(8,128)S(1)}, u32[]{:S(2)}, u32[]{:S(2)}) collective-permute-start(f32[32,6144]{1,0:T(8,128)} %bitcast.10), channel_id=1, source_target_pairs={{0,4},{1,5},{2,6},{3,7},{4,8},{5,9},{6,10},{7,11},{8,12},{9,13},{1... | collective-permute-start | bytes 2359304 | tf_op jit(solution)/shard_map/ppermute | solution.py:34
  3.3 23.4 %collective-permute-start.9 = (f32[32,6144]{1,0:T(8,128)}, f32[32,6144]{1,0:T(8,128)S(1)}, u32[]{:S(2)}, u32[]{:S(2)}) collective-permute-start(f32[32,6144]{1,0:T(8,128)} %bitcast.11), channel_id=1, source_target_pairs={{0,12},{1,3},{2,14},{3,1},{4,0},{5,7},{6,2},{7,5},{8,4},{9,11},{10... | collective-permute-start | bytes 2359304 | tf_op jit(solution)/shard_map/ppermute | solution.py:34
  4.6 37.1 %collective-permute-start.1 = (f32[32,6144]{1,0:T(8,128)}, f32[32,6144]{1,0:T(8,128)S(1)}, u32[]{:S(2)}, u32[]{:S(2)}) collective-permute-start(f32[32,6144]{1,0:T(8,128)} %param.5), channel_id=1, source_target_pairs={{0,2},{1,13},{2,0},{3,15},{4,6},{5,1},{6,4},{7,3},{8,10},{9,5},{10... | collective-permute-start | bytes 2359304 | tf_op jit(solution)/shard_map/ppermute | solution.py:34
  7.3 33.5 %collective-permute-start = (f32[32,6144]{1,0:T(8,128)}, f32[32,6144]{1,0:T(8,128)S(1)}, u32[]{:S(2)}, u32[]{:S(2)}) collective-permute-start(f32[32,6144]{1,0:T(8,128)} %param.5), channel_id=1, source_target_pairs={{0,4},{1,5},{2,6},{3,7},{4,8},{5,9},{6,10},{7,11},{8,12},{9,13},{1... | collective-permute-start | bytes 2359304 | tf_op jit(solution)/shard_map/ppermute | solution.py:34
  23.9 19.6 %collective-permute-start.2 = (f32[32,6144]{1,0:T(8,128)S(1)}, f32[32,6144]{1,0:T(8,128)S(1)}, u32[]{:S(2)}, u32[]{:S(2)}) collective-permute-start(f32[32,6144]{1,0:T(8,128)S(1)} %copy-done.2), channel_id=1, source_target_pairs={{0,12},{1,3},{2,14},{3,1},{4,0},{5,7},{6,2},{7,5},{8,4},{9,11},{10... | collective-permute-start | bytes 2359304 | tf_op jit(solution)/shard_map/ppermute | solution.py:34
  24.8 57.3 %collective-permute-start.14 = (f32[6144,128]{1,0:T(8,128)S(1)}, f32[6144,128]{1,0:T(8,128)S(1)}, u32[]{:S(2)}, u32[]{:S(2)}) collective-permute-start(f32[6144,128]{1,0:T(8,128)S(1)} %copy-done), channel_id=1, source_target_pairs={{0,1},{1,0},{2,3},{3,2},{4,5},{5,4},{6,7},{7,6},{8,9},{9,8},{10,11... | collective-permute-start | bytes 9437192 | tf_op jit(solution)/shard_map/ppermute | solution.py:47
  26.7 21.7 %collective-permute-start.10 = (f32[32,6144]{1,0:T(8,128)S(1)}, f32[32,6144]{1,0:T(8,128)S(1)}, u32[]{:S(2)}, u32[]{:S(2)}) collective-permute-start(f32[32,6144]{1,0:T(8,128)S(1)} %collective-permute-done.8), channel_id=1, source_target_pairs={{0,4},{1,3},{2,6},{3,1},{4,8},{5,7},{6,10},{7,5},{8,12},{9,11},{10... | collective-permute-start | bytes 2359304 | tf_op jit(solution)/shard_map/ppermute | solution.py:34
  40.8 18.3 %collective-permute-start.11 = (f32[32,6144]{1,0:T(8,128)S(1)}, f32[32,6144]{1,0:T(8,128)S(1)}, u32[]{:S(2)}, u32[]{:S(2)}) collective-permute-start(f32[32,6144]{1,0:T(8,128)S(1)} %collective-permute-done.8), channel_id=1, source_target_pairs={{0,12},{1,13},{2,14},{3,15},{4,0},{5,1},{6,2},{7,3},{8,4},{9,5},{1... | collective-permute-start | bytes 2359304 | tf_op jit(solution)/shard_map/ppermute | solution.py:34
  41.7 36.5 %collective-permute-start.12 = (f32[32,6144]{1,0:T(8,128)S(1)}, f32[32,6144]{1,0:T(8,128)S(1)}, u32[]{:S(2)}, u32[]{:S(2)}) collective-permute-start(f32[32,6144]{1,0:T(8,128)S(1)} %collective-permute-done.7), channel_id=1, source_target_pairs={{0,4},{1,3},{2,6},{3,1},{4,8},{5,7},{6,10},{7,5},{8,12},{9,11},{10... | collective-permute-start | bytes 2359304 | tf_op jit(solution)/shard_map/ppermute | solution.py:34
  43.5 21.7 %collective-permute-start.3 = (f32[32,6144]{1,0:T(8,128)S(1)}, f32[32,6144]{1,0:T(8,128)S(1)}, u32[]{:S(2)}, u32[]{:S(2)}) collective-permute-start(f32[32,6144]{1,0:T(8,128)S(1)} %collective-permute-done.1), channel_id=1, source_target_pairs={{0,4},{1,3},{2,6},{3,1},{4,8},{5,7},{6,10},{7,5},{8,12},{9,11},{10... | collective-permute-start | bytes 2359304 | tf_op jit(solution)/shard_map/ppermute | solution.py:34
  48.4 27.6 %collective-permute-start.4 = (f32[32,6144]{1,0:T(8,128)S(1)}, f32[32,6144]{1,0:T(8,128)S(1)}, u32[]{:S(2)}, u32[]{:S(2)}) collective-permute-start(f32[32,6144]{1,0:T(8,128)S(1)} %collective-permute-done.1), channel_id=1, source_target_pairs={{0,12},{1,13},{2,14},{3,15},{4,0},{5,1},{6,2},{7,3},{8,4},{9,5},{1... | collective-permute-start | bytes 2359304 | tf_op jit(solution)/shard_map/ppermute | solution.py:34
  59.1 36.5 %collective-permute-start.5 = (f32[32,6144]{1,0:T(8,128)S(1)}, f32[32,6144]{1,0:T(8,128)S(1)}, u32[]{:S(2)}, u32[]{:S(2)}) collective-permute-start(f32[32,6144]{1,0:T(8,128)S(1)} %collective-permute-done), channel_id=1, source_target_pairs={{0,4},{1,3},{2,6},{3,1},{4,8},{5,7},{6,10},{7,5},{8,12},{9,11},{10... | collective-permute-start | bytes 2359304 | tf_op jit(solution)/shard_map/ppermute | solution.py:34
  65.2 16.9 %collective-permute-start.13 = (f32[32,6144]{1,0:T(8,128)S(1)}, f32[32,6144]{1,0:T(8,128)S(1)}, u32[]{:S(2)}, u32[]{:S(2)}) collective-permute-start(f32[32,6144]{1,0:T(8,128)S(1)} %collective-permute-done.11), channel_id=1, source_target_pairs={{0,12},{1,3},{2,14},{3,1},{4,0},{5,7},{6,2},{7,5},{8,4},{9,11},{10... | collective-permute-start | bytes 2359304 | tf_op jit(solution)/shard_map/ppermute | solution.py:34
  76.0 33.7 %collective-permute-start.6 = (f32[32,6144]{1,0:T(8,128)S(1)}, f32[32,6144]{1,0:T(8,128)S(1)}, u32[]{:S(2)}, u32[]{:S(2)}) collective-permute-start(f32[32,6144]{1,0:T(8,128)S(1)} %collective-permute-done.4), channel_id=1, source_target_pairs={{0,12},{1,3},{2,14},{3,1},{4,0},{5,7},{6,2},{7,5},{8,4},{9,11},{10... | collective-permute-start | bytes 2359304 | tf_op jit(solution)/shard_map/ppermute | solution.py:34
  86.0 18.8 %all-to-all-start = ((f32[16,16,256]{2,1,0:T(8,128)}), f32[16,16,256]{2,1,0:T(8,128)S(1)}, u32[]{:S(2)}, u32[]{:S(2)}) async-start(f32[16,16,256]{2,1,0:T(8,128)} %bitcast.1), calls=%async_computation | async-start | bytes 524288 | tf_op jit(solution)/shard_map/all_to_all | solution.py:60
  105.6 13.3 %all-to-all-start.1 = ((f32[16,16,256]{2,1,0:T(8,128)}), f32[16,16,256]{2,1,0:T(8,128)S(1)}, u32[]{:S(2)}, u32[]{:S(2)}) async-start(f32[16,16,256]{2,1,0:T(8,128)} %broadcast_in_dim.4), calls=%async_computation.1 | async-start | bytes 524288 | tf_op jit(solution)/shard_map/all_to_all | solution.py:63
  123.5 18.7 %copy-start.1 = (f32[6144,128]{1,0:T(8,128)S(1)}, f32[6144,128]{1,0:T(8,128)}, u32[]{:S(2)}) copy-start(f32[6144,128]{1,0:T(8,128)} %param.7) | copy-start | bytes 9437188
  128.4 11.6 %collective-permute-start.16 = (f32[3072,128]{1,0:T(8,128)S(1)}, f32[3072,128]{1,0:T(8,128)S(1)}, u32[]{:S(2)}, u32[]{:S(2)}) collective-permute-start(f32[3072,128]{1,0:T(8,128)S(1)} %slice.37), channel_id=1, source_target_pairs={{0,1},{1,0},{2,3},{3,2},{4,5},{5,4},{6,7},{7,6},{8,9},{9,8},{10,11... | collective-permute-start | bytes 4718600 | tf_op jit(solution)/shard_map/ppermute | solution.py:47
  137.1 5.2 %collective-permute-start.15 = (f32[3072,128]{1,0:T(8,128)S(1)}, f32[3072,128]{1,0:T(8,128)S(1)}, u32[]{:S(2)}, u32[]{:S(2)}) collective-permute-start(f32[3072,128]{1,0:T(8,128)S(1)} %slice.34), channel_id=1, source_target_pairs={{0,1},{1,0},{2,3},{3,2},{4,5},{5,4},{6,7},{7,6},{8,9},{9,8},{10,11... | collective-permute-start | bytes 4718600 | tf_op jit(solution)/shard_map/ppermute | solution.py:47

commit v2 on v1

--- a/solution.py
+++ b/solution.py
@@ -4,15 +4,15 @@
 from jax.sharding import PartitionSpec as P
 
 ROUTES = (
-    (0, "+", "+"),
-    (0, "y", "-"),
-    (0, "-", "y"),
-    (2, "+", "y"),
-    (2, "-", "-"),
-    (1, "+", "y"),
-    (5, "-", "y"),
+    (0, "+", "-"),
+    (0, "-", "+"),
+    (0, "y", "y"),
+    (1, "+", "-"),
+    (2, "y", "y"),
+    (3, "+", "-"),
+    (6, "+", "-"),
 )
-C_CHUNKS = 2
+C_CHUNKS = 3
 
 
 def target(at, move):
@@ -53,14 +53,18 @@
 
 def on_device(a_panel, u_rows, u_col, c_in):
     other_col = swapped(u_col)
-    a = jnp.concatenate(gather_blocks(a_panel.T), axis=0)
+    a = gather_blocks(a_panel.T)
     u = gather_blocks(u_rows)
-    partial = product(a, jnp.concatenate([u_col, other_col], axis=1))
-    tiles = partial.reshape(16, partial.shape[0] // 16, partial.shape[1])
-    tiles = lax.all_to_all(tiles, "prow", 0, 0, tiled=True)
-    share = jnp.sum(tiles, axis=0)
-    copies = jnp.broadcast_to(share, tiles.shape)
-    inner = lax.all_to_all(copies, "prow", 0, 0, tiled=True).reshape(partial.shape)
+    u_cols = jnp.concatenate([u_col, other_col], axis=1)
+    shares = []
+    for half in range(2):
+        part = product(jnp.concatenate(a[half * 4 : half * 4 + 4], axis=0), u_cols)
+        tiles = part.reshape(16, part.shape[0] // 16, part.shape[1])
+        tiles = lax.all_to_all(tiles, "prow", 0, 0, tiled=True)
+        shares.append(jnp.sum(tiles, axis=0))
+    copies = jnp.broadcast_to(jnp.stack(shares), (16, 2, *shares[0].shape))
+    inner = lax.all_to_all(copies, "prow", 0, 0, tiled=True)
+    inner = jnp.moveaxis(inner, 1, 0).reshape(-1, inner.shape[-1])
     u = placed_blocks(u)
     rows, width = c_in.shape[0] // C_CHUNKS, c_in.shape[1]
     done = []

time: 145 us -> 155 us (1.069)
  starting transfers between devices: 36.1 us -> 50.5 us
  waiting for transfers between devices: 79.2 us -> 72.5 us
  matrix products: 13.2 us -> 18.4 us
  local copies, waits for them, and re-layouts: 13.6 us -> 10.1 us
    ppermute x14, starting transfers between devices: 12 us -> 21.4 us  [gather_blocks(): held.append(lax.ppermute(held[source], 'pcol', pairs(moves)))]
    ppermute x14, waiting for transfers between devices: 57.5 us -> 50.3 us  [gather_blocks(): held.append(lax.ppermute(held[source], 'pcol', pairs(moves)))]
    all_to_all x1 -> x2, starting transfers between devices: 9.57 us -> 16.2 us  [on_device(): tiles = lax.all_to_all(tiles, 'prow', 0, 0, tiled=True)]
    dot_general x3 -> x5, matrix products: 13.2 us -> 18.4 us  [product(): jnp.dot(a, b, precision=lax.Precision.HIGH, preferred_element_type=jnp.fl...]
    dynamic_update_slice x8, local copies, waits for them, and re-layouts: 11.1 us -> 6.24 us  [placed_blocks(): out = lax.dynamic_update_slice(out, block, (i * k, 0))]
    all_to_all x1 -> x2, waiting for transfers between devices: 8.3 us -> 10.6 us  [on_device(): tiles = lax.all_to_all(tiles, 'prow', 0, 0, tiled=True)]
    ppermute x3 -> x4, starting transfers between devices: 10.5 us -> 9.35 us  [swapped(): return lax.ppermute(x, 'pcol', [(at, at ^ 1) for at in range(16)])]
    ppermute x3 -> x4, waiting for transfers between devices: 5.08 us -> 4.46 us  [swapped(): return lax.ppermute(x, 'pcol', [(at, at ^ 1) for at in range(16)])]
  transfers between devices with their start and end apart: 19 -> 21, of which waited for: 11 -> 14; matrix products, arithmetic and copies ran while one was open for 12% -> 10% of each run, Pallas kernels for 0% -> 0%
where the time goes in v2:
time: 155 us; the launch traced here: 154 us
  waiting for transfers between devices  72.5 us (47%)
  starting transfers between devices  50.5 us (33%)
  matrix products  18.4 us (12%)
  local copies, waits for them, and re-layouts  10.1 us (7%)
  other arithmetic  2.35 us (2%)
    ppermute x14, waiting for transfers between devices, gather_blocks(): held.append(lax.ppermute(held[source], 'pcol', pairs(moves)))  50.3 us
    ppermute x14, starting transfers between devices, gather_blocks(): held.append(lax.ppermute(held[source], 'pcol', pairs(moves)))  21.4 us
    dot_general x5, matrix products, product(): jnp.dot(a, b, precision=lax.Precision.HIGH, preferred_element_type=jnp.fl...  18.4 us
    all_to_all x2, starting transfers between devices, on_device(): tiles = lax.all_to_all(tiles, 'prow', 0, 0, tiled=True)  16.2 us
    all_to_all x2, waiting for transfers between devices, on_device(): tiles = lax.all_to_all(tiles, 'prow', 0, 0, tiled=True)  10.6 us
    ppermute x4, starting transfers between devices, swapped(): return lax.ppermute(x, 'pcol', [(at, at ^ 1) for at in range(16)])  9.35 us
    all_to_all x1, waiting for transfers between devices, on_device(): inner = lax.all_to_all(copies, 'prow', 0, 0, tiled=True)  7.24 us
    dynamic_update_slice x8, local copies, waits for them, and re-layouts, placed_blocks(): out = lax.dynamic_update_slice(out, block, (i * k, 0))  6.24 us
  transfers between devices with their start and end apart: 21, of which 14 were waited for; matrix products, arithmetic and copies ran while one was open for 10% of the time, Pallas kernels for 0%

profile of v2, /device:TPU:1, one launch (start us, length us, event | category | flops | bytes accessed | tf_op | source)
XLA Modules:
  0.0 154.1 jit_solution(11775025734874110443)
XLA Ops:
  0.0 3.3 %collective-permute-start = (f32[32,6144]{1,0:T(8,128)}, f32[32,6144]{1,0:T(8,128)S(1)}, u32[]{:S(2)}, u32[]{:S(2)}) collective-permute-start(f32[32,6144]{1,0:T(8,128)} %param.5), channel_id=1, source_target_pairs={{0,4},{1,13},{2,6},{3,15},{4,8},{5,1},{6,10},{7,3},{8,12},{9,5},{1... | collective-permute-start | bytes 2359304 | tf_op jit(solution)/shard_map/ppermute | solution.py:34
  4.8 3.1 %collective-permute-start.10 = (f32[6144,128]{1,0:T(8,128)}, f32[6144,128]{1,0:T(8,128)S(1)}, u32[]{:S(2)}, u32[]{:S(2)}) collective-permute-start(f32[6144,128]{1,0:T(8,128)} %param.6), channel_id=1, source_target_pairs={{0,1},{1,0},{2,3},{3,2},{4,5},{5,4},{6,7},{7,6},{8,9},{9,8},{10,11... | collective-permute-start | bytes 9437192 | tf_op jit(solution)/shard_map/ppermute | solution.py:47
  7.9 1.8 %dynamic_update_slice.24 = f32[256,6144]{1,0:T(8,128)S(1)} pad(f32[32,6144]{1,0:T(8,128)} %param.5, f32[]{:T(128)} %constant.9.clone.1), padding=0_224x0_0 | pad | bytes 7077892 | tf_op jit(solution)/shard_map/dynamic_update_slice | solution.py:42
  10.0 7.7 %collective-permute-done = f32[32,6144]{1,0:T(8,128)S(1)} collective-permute-done((f32[32,6144]{1,0:T(8,128)}, f32[32,6144]{1,0:T(8,128)S(1)}, u32[]{:S(2)}, u32[]{:S(2)}) %collective-permute-start) | collective-permute-done | bytes 786464 | tf_op jit(solution)/shard_map/ppermute | solution.py:34
  17.7 3.0 %collective-permute-start.2 = (f32[32,6144]{1,0:T(8,128)S(1)}, f32[32,6144]{1,0:T(8,128)S(1)}, u32[]{:S(2)}, u32[]{:S(2)}) collective-permute-start(f32[32,6144]{1,0:T(8,128)S(1)} %copy-done.4), channel_id=1, source_target_pairs={{0,2},{1,3},{2,0},{3,1},{4,6},{5,7},{6,4},{7,5},{8,10},{9,11},{10,... | collective-permute-start | bytes 2359304 | tf_op jit(solution)/shard_map/ppermute | solution.py:34
  20.7 3.3 %collective-permute-done.1 = f32[32,6144]{1,0:T(8,128)S(1)} collective-permute-done((f32[32,6144]{1,0:T(8,128)}, f32[32,6144]{1,0:T(8,128)S(1)}, u32[]{:S(2)}, u32[]{:S(2)}) %collective-permute-start.1) | collective-permute-done | bytes 786464 | tf_op jit(solution)/shard_map/ppermute | solution.py:34
  25.1 10.8 %collective-permute-done.8 = f32[32,6144]{1,0:T(8,128)S(1)} collective-permute-done((f32[32,6144]{1,0:T(8,128)}, f32[32,6144]{1,0:T(8,128)S(1)}, u32[]{:S(2)}, u32[]{:S(2)}) %collective-permute-start.8) | collective-permute-done | bytes 786464 | tf_op jit(solution)/shard_map/ppermute | solution.py:34
  35.9 4.7 %collective-permute-start.13 = (f32[32,6144]{1,0:T(8,128)S(1)}, f32[32,6144]{1,0:T(8,128)S(1)}, u32[]{:S(2)}, u32[]{:S(2)}) collective-permute-start(f32[32,6144]{1,0:T(8,128)S(1)} %collective-permute-done.9), channel_id=1, source_target_pairs={{0,4},{1,13},{2,6},{3,15},{4,8},{5,1},{6,10},{7,3},{8,12},{9,5},{1... | collective-permute-start | bytes 2359304 | tf_op jit(solution)/shard_map/ppermute | solution.py:34
  41.0 5.2 %collective-permute-done.7 = f32[32,6144]{1,0:T(8,128)S(1)} collective-permute-done((f32[32,6144]{1,0:T(8,128)S(1)}, f32[32,6144]{1,0:T(8,128)S(1)}, u32[]{:S(2)}, u32[]{:S(2)}) %collective-permute-start.7) | collective-permute-done | bytes 786464 | tf_op jit(solution)/shard_map/ppermute | solution.py:34
  47.4 7.1 %collective-permute-done.13 = f32[32,6144]{1,0:T(8,128)S(1)} collective-permute-done((f32[32,6144]{1,0:T(8,128)S(1)}, f32[32,6144]{1,0:T(8,128)S(1)}, u32[]{:S(2)}, u32[]{:S(2)}) %collective-permute-start.13) | collective-permute-done | bytes 786464 | tf_op jit(solution)/shard_map/ppermute | solution.py:34
  54.6 3.1 %collective-permute-start.11 = (f32[32,6144]{1,0:T(8,128)S(1)}, f32[32,6144]{1,0:T(8,128)S(1)}, u32[]{:S(2)}, u32[]{:S(2)}) collective-permute-start(f32[32,6144]{1,0:T(8,128)S(1)} %collective-permute-done.7), channel_id=1, source_target_pairs={{0,4},{1,13},{2,6},{3,15},{4,8},{5,1},{6,10},{7,3},{8,12},{9,5},{1... | collective-permute-start | bytes 2359304 | tf_op jit(solution)/shard_map/ppermute | solution.py:34
  57.7 5.3 %collective-permute-done.5 = f32[32,6144]{1,0:T(8,128)} collective-permute-done((f32[32,6144]{1,0:T(8,128)S(1)}, f32[32,6144]{1,0:T(8,128)}, u32[]{:S(2)}, u32[]{:S(2)}) %collective-permute-start.5) | collective-permute-done | bytes 786464 | tf_op jit(solution)/shard_map/ppermute | solution.py:34
  63.0 3.2 %collective-permute-start.6 = (f32[32,6144]{1,0:T(8,128)}, f32[32,6144]{1,0:T(8,128)}, u32[]{:S(2)}, u32[]{:S(2)}) collective-permute-start(f32[32,6144]{1,0:T(8,128)} %collective-permute-done.5), channel_id=1, source_target_pairs={{0,4},{1,13},{2,6},{3,15},{4,8},{5,1},{6,10},{7,3},{8,12},{9,5},{1... | collective-permute-start | bytes 2359304 | tf_op jit(solution)/shard_map/ppermute | solution.py:34
  66.6 2.4 %copy-done.1 = f32[256,6144]{1,0:T(8,128)} copy-done((f32[256,6144]{1,0:T(8,128)}, f32[256,6144]{1,0:T(8,128)S(1)}, u32[]{:S(2)}) %copy-start.1) | copy-done | bytes 6291480
  68.9 3.4 %collective-permute-done.12 = f32[32,6144]{1,0:T(8,128)S(1)} collective-permute-done((f32[32,6144]{1,0:T(8,128)S(1)}, f32[32,6144]{1,0:T(8,128)S(1)}, u32[]{:S(2)}, u32[]{:S(2)}) %collective-permute-start.12) | collective-permute-done | bytes 786464 | tf_op jit(solution)/shard_map/ppermute | solution.py:34
  72.3 7.5 %collective-permute-done.14 = f32[32,6144]{1,0:T(8,128)S(1)} collective-permute-done((f32[32,6144]{1,0:T(8,128)S(1)}, f32[32,6144]{1,0:T(8,128)S(1)}, u32[]{:S(2)}, u32[]{:S(2)}) %collective-permute-start.14) | collective-permute-done | bytes 786464 | tf_op jit(solution)/shard_map/ppermute | solution.py:34
  79.9 2.9 %fusion.22 = f32[16,8,256]{2,1,0:T(8,128)} fusion(f32[6144,256]{1,0:T(8,128)S(1)} %constant_dynamic-update-slice_fusion, f32[32,6144]{1,0:T(8,128)S(1)} %collective-permute-done.14, f32[32,6144]{1,0:T(8,128)S(1)} %collective-permute-done.13, f32[32,6144]{1,0:T(8,128)S(1)} %collective-permute-done.12, f32[32,6144]{1,0:T(8,128)S(1)} %collective-permute-done.11), kind=kOutput, calls=%fused_computation.23 | convolution fusion | flops 1210318848 | bytes 9568256 | tf_op jit(solution)/shard_map/dot_general | solution.py:51
  82.7 10.9 %all-to-all-start.1 = ((f32[16,8,256]{2,1,0:T(8,128)}), f32[16,8,256]{2,1,0:T(8,128)S(1)}, u32[]{:S(2)}, u32[]{:S(2)}) async-start(f32[16,8,256]{2,1,0:T(8,128)} %fusion.22), calls=%async_computation.1 | async-start | bytes 262144 | tf_op jit(solution)/shard_map/all_to_all | solution.py:63
  93.7 5.2 %fusion.25 = f32[16,8,256]{2,1,0:T(8,128)} fusion(f32[6144,256]{1,0:T(8,128)} %copy-done, f32[32,6144]{1,0:T(8,128)S(1)} %collective-permute-done.9, f32[32,6144]{1,0:T(8,128)S(1)} %collective-permute-done.8, f32[32,6144]{1,0:T(8,128)S(1)} %collective-permute-done.7, f32[32,6144]{1,0:T(8,128)S(1)} %bitcast.21), kind=kOutput, calls=%fused_computation.24 | convolution fusion | flops 1210318848 | bytes 9568256 | tf_op jit(solution)/shard_map/dot_general | solution.py:51
  98.8 3.8 %all-to-all-done.1 = f32[16,8,256]{2,1,0:T(8,128)S(1)} async-done(((f32[16,8,256]{2,1,0:T(8,128)}), f32[16,8,256]{2,1,0:T(8,128)S(1)}, u32[]{:S(2)}, u32[]{:S(2)}) %all-to-all-start.1) | async-done | bytes 131104 | tf_op jit(solution)/shard_map/all_to_all | solution.py:63
  102.6 5.3 %all-to-all-start = ((f32[16,8,256]{2,1,0:T(8,128)}), f32[16,8,256]{2,1,0:T(8,128)S(1)}, u32[]{:S(2)}, u32[]{:S(2)}) async-start(f32[16,8,256]{2,1,0:T(8,128)} %fusion.25), calls=%async_computation | async-start | bytes 262144 | tf_op jit(solution)/shard_map/all_to_all | solution.py:63
  107.9 2.1 %constant_dynamic-update-slice_fusion.3 = f32[256,6144]{1,0:T(8,128)} fusion(f32[256,6144]{1,0:T(8,128)} %copy-done.1, f32[32,6144]{1,0:T(8,128)} %collective-permute-done.5), kind=kLoop, calls=%fused_computation.35 | loop fusion | bytes 1572864 | tf_op jit(solution)/shard_map/dynamic_update_slice | solution.py:42
  110.0 6.8 %all-to-all-done = f32[16,8,256]{2,1,0:T(8,128)S(1)} async-done(((f32[16,8,256]{2,1,0:T(8,128)}), f32[16,8,256]{2,1,0:T(8,128)S(1)}, u32[]{:S(2)}, u32[]{:S(2)}) %all-to-all-start) | async-done | bytes 131104 | tf_op jit(solution)/shard_map/all_to_all | solution.py:63
  117.6 3.5 %all-to-all-start.2 = ((f32[16,2,8,256]{3,2,1,0:T(8,128)}), f32[16,2,8,256]{3,2,1,0:T(8,128)S(1)}, u32[]{:S(2)}, u32[]{:S(2)}) async-start(f32[16,2,8,256]{3,2,1,0:T(8,128)} %broadcast_in_dim.4), calls=%async_computation.2 | async-start | bytes 524288 | tf_op jit(solution)/shard_map/all_to_all | solution.py:66
  121.1 2.1 %constant_dynamic-update-slice_fusion.2 = f32[256,6144]{1,0:T(8,128)} fusion(f32[256,6144]{1,0:T(8,128)} %constant_dynamic-update-slice_fusion.3, f32[32,6144]{1,0:T(8,128)} %collective-permute-done.6), kind=kLoop, calls=%fused_computation.34 | loop fusion | bytes 1572864 | tf_op jit(solution)/shard_map/dynamic_update_slice | solution.py:42
  123.2 7.2 %all-to-all-done.2 = f32[16,2,8,256]{3,2,1,0:T(8,128)S(1)} async-done(((f32[16,2,8,256]{3,2,1,0:T(8,128)}), f32[16,2,8,256]{3,2,1,0:T(8,128)S(1)}, u32[]{:S(2)}, u32[]{:S(2)}) %all-to-all-start.2) | async-done | bytes 262176 | tf_op jit(solution)/shard_map/all_to_all | solution.py:66
  130.5 3.4 %fusion.20 = f32[2048,256]{1,0:T(8,128)S(1)} fusion(f32[256,256]{1,0:T(8,128)S(1)} %bitcast.15, f32[256,6144]{1,0:T(8,128)} %constant_dynamic-update-slice_fusion.2), kind=kOutput, calls=%fused_computation.21 | convolution fusion | flops 805306368 | bytes 4456448 | tf_op jit(solution)/shard_map/dot_general | solution.py:51
  133.9 3.4 %fusion.16 = f32[2048,256]{1,0:T(8,128)S(1)} fusion(f32[256,256]{1,0:T(8,128)S(1)} %bitcast.16, f32[256,6144]{1,0:T(8,128)} %constant_dynamic-update-slice_fusion.2), kind=kOutput, calls=%fused_computation.17 | convolution fusion | flops 805306368 | bytes 4456448 | tf_op jit(solution)/shard_map/dot_general | solution.py:51
  137.4 3.4 %fusion.18 = f32[2048,256]{1,0:T(8,128)S(1)} fusion(f32[256,256]{1,0:T(8,128)S(1)} %bitcast.17, f32[256,6144]{1,0:T(8,128)} %constant_dynamic-update-slice_fusion.2), kind=kOutput, calls=%fused_computation.19 | convolution fusion | flops 805306368 | bytes 4456448 | tf_op jit(solution)/shard_map/dot_general | solution.py:51
  140.9 5.6 %collective-permute-start.15 = (f32[2048,128]{1,0:T(8,128)S(1)}, f32[2048,128]{1,0:T(8,128)S(1)}, u32[]{:S(2)}, u32[]{:S(2)}) collective-permute-start(f32[2048,128]{1,0:T(8,128)S(1)} %slice.50), channel_id=1, source_target_pairs={{0,1},{1,0},{2,3},{3,2},{4,5},{5,4},{6,7},{7,6},{8,9},{9,8},{10,11... | collective-permute-start | bytes 3145736 | tf_op jit(solution)/shard_map/ppermute | solution.py:47
  150.3 1.5 collective-permute-done.16
  152.2 1.9 %pad_maximum_fusion = f32[6144,128]{1,0:T(8,128)} fusion(f32[2048,128]{1,0:T(8,128)S(1)} %get-tuple-element.6, f32[2048,128]{1,0:T(8,128)S(1)} %get-tuple-element.7, f32[2048,128]{1,0:T(8,128)S(1)} %get-tuple-element.5), kind=kLoop, calls=%fused_computation.16 | loop fusion | flops 1572864 | bytes 6291456 | tf_op jit(solution)/shard_map/concatenate | solution.py:75
  (47 shorter events, 10.0 us)
Async XLA Ops:
  0.0 17.6 %collective-permute-start = (f32[32,6144]{1,0:T(8,128)}, f32[32,6144]{1,0:T(8,128)S(1)}, u32[]{:S(2)}, u32[]{:S(2)}) collective-permute-start(f32[32,6144]{1,0:T(8,128)} %param.5), channel_id=1, source_target_pairs={{0,4},{1,13},{2,6},{3,15},{4,8},{5,1},{6,10},{7,3},{8,12},{9,5},{1... | collective-permute-start | bytes 2359304 | tf_op jit(solution)/shard_map/ppermute | solution.py:34
  3.3 20.6 %collective-permute-start.1 = (f32[32,6144]{1,0:T(8,128)}, f32[32,6144]{1,0:T(8,128)S(1)}, u32[]{:S(2)}, u32[]{:S(2)}) collective-permute-start(f32[32,6144]{1,0:T(8,128)} %param.5), channel_id=1, source_target_pairs={{0,12},{1,5},{2,14},{3,7},{4,0},{5,9},{6,2},{7,11},{8,4},{9,13},{1... | collective-permute-start | bytes 2359304 | tf_op jit(solution)/shard_map/ppermute | solution.py:34
  3.3 6.4 %copy-start.2 = (f32[6144,128]{1,0:T(8,128)S(1)}, f32[6144,128]{1,0:T(8,128)}, u32[]{:S(2)}) copy-start(f32[6144,128]{1,0:T(8,128)} %param.6) | copy-start | bytes 9437188
  3.3 20.8 %collective-permute-start.9 = (f32[32,6144]{1,0:T(8,128)}, f32[32,6144]{1,0:T(8,128)S(1)}, u32[]{:S(2)}, u32[]{:S(2)}) collective-permute-start(f32[32,6144]{1,0:T(8,128)} %bitcast.18), channel_id=1, source_target_pairs={{0,2},{1,3},{2,0},{3,1},{4,6},{5,7},{6,4},{7,5},{8,10},{9,11},{10,... | collective-permute-start | bytes 2359304 | tf_op jit(solution)/shard_map/ppermute | solution.py:34
  4.6 31.3 %collective-permute-start.8 = (f32[32,6144]{1,0:T(8,128)}, f32[32,6144]{1,0:T(8,128)S(1)}, u32[]{:S(2)}, u32[]{:S(2)}) collective-permute-start(f32[32,6144]{1,0:T(8,128)} %bitcast.19), channel_id=1, source_target_pairs={{0,12},{1,5},{2,14},{3,7},{4,0},{5,9},{6,2},{7,11},{8,4},{9,13},{1... | collective-permute-start | bytes 2359304 | tf_op jit(solution)/shard_map/ppermute | solution.py:34
  4.8 61.5 %collective-permute-start.10 = (f32[6144,128]{1,0:T(8,128)}, f32[6144,128]{1,0:T(8,128)S(1)}, u32[]{:S(2)}, u32[]{:S(2)}) collective-permute-start(f32[6144,128]{1,0:T(8,128)} %param.6), channel_id=1, source_target_pairs={{0,1},{1,0},{2,3},{3,2},{4,5},{5,4},{6,7},{7,6},{8,9},{9,8},{10,11... | collective-permute-start | bytes 9437192 | tf_op jit(solution)/shard_map/ppermute | solution.py:47
  9.7 8.0 %copy-start.4 = (f32[32,6144]{1,0:T(8,128)S(1)}, f32[32,6144]{1,0:T(8,128)}, u32[]{:S(2)}) copy-start(f32[32,6144]{1,0:T(8,128)} %param.5) | copy-start | bytes 2359300
  9.7 14.4 %copy-start.5 = (f32[6144,32]{0,1:T(8,128)S(1)}, f32[6144,32]{0,1:T(8,128)}, u32[]{:S(2)}) copy-start(f32[6144,32]{0,1:T(8,128)} %param.4) | copy-start | bytes 2359300
  17.7 18.3 %collective-permute-start.2 = (f32[32,6144]{1,0:T(8,128)S(1)}, f32[32,6144]{1,0:T(8,128)S(1)}, u32[]{:S(2)}, u32[]{:S(2)}) collective-permute-start(f32[32,6144]{1,0:T(8,128)S(1)} %copy-done.4), channel_id=1, source_target_pairs={{0,2},{1,3},{2,0},{3,1},{4,6},{5,7},{6,4},{7,5},{8,10},{9,11},{10,... | collective-permute-start | bytes 2359304 | tf_op jit(solution)/shard_map/ppermute | solution.py:34
  23.9 16.7 %collective-permute-start.3 = (f32[32,6144]{1,0:T(8,128)S(1)}, f32[32,6144]{1,0:T(8,128)S(1)}, u32[]{:S(2)}, u32[]{:S(2)}) collective-permute-start(f32[32,6144]{1,0:T(8,128)S(1)} %collective-permute-done), channel_id=1, source_target_pairs={{0,4},{1,13},{2,6},{3,15},{4,8},{5,1},{6,10},{7,3},{8,12},{9,5},{1... | collective-permute-start | bytes 2359304 | tf_op jit(solution)/shard_map/ppermute | solution.py:34
  24.1 22.0 %collective-permute-start.7 = (f32[32,6144]{1,0:T(8,128)S(1)}, f32[32,6144]{1,0:T(8,128)S(1)}, u32[]{:S(2)}, u32[]{:S(2)}) collective-permute-start(f32[32,6144]{1,0:T(8,128)S(1)} %bitcast.20), channel_id=1, source_target_pairs={{0,4},{1,13},{2,6},{3,15},{4,8},{5,1},{6,10},{7,3},{8,12},{9,5},{1... | collective-permute-start | bytes 2359304 | tf_op jit(solution)/shard_map/ppermute | solution.py:34
  35.9 21.8 %collective-permute-start.4 = (f32[32,6144]{1,0:T(8,128)S(1)}, f32[32,6144]{1,0:T(8,128)S(1)}, u32[]{:S(2)}, u32[]{:S(2)}) collective-permute-start(f32[32,6144]{1,0:T(8,128)S(1)} %collective-permute-done.1), channel_id=1, source_target_pairs={{0,2},{1,3},{2,0},{3,1},{4,6},{5,7},{6,4},{7,5},{8,10},{9,11},{10,... | collective-permute-start | bytes 2359304 | tf_op jit(solution)/shard_map/ppermute | solution.py:34
  35.9 18.7 %collective-permute-start.13 = (f32[32,6144]{1,0:T(8,128)S(1)}, f32[32,6144]{1,0:T(8,128)S(1)}, u32[]{:S(2)}, u32[]{:S(2)}) collective-permute-start(f32[32,6144]{1,0:T(8,128)S(1)} %collective-permute-done.9), channel_id=1, source_target_pairs={{0,4},{1,13},{2,6},{3,15},{4,8},{5,1},{6,10},{7,3},{8,12},{9,5},{1... | collective-permute-start | bytes 2359304 | tf_op jit(solution)/shard_map/ppermute | solution.py:34
  40.6 22.4 %collective-permute-start.5 = (f32[32,6144]{1,0:T(8,128)S(1)}, f32[32,6144]{1,0:T(8,128)}, u32[]{:S(2)}, u32[]{:S(2)}) collective-permute-start(f32[32,6144]{1,0:T(8,128)S(1)} %collective-permute-done.2), channel_id=1, source_target_pairs={{0,4},{1,13},{2,6},{3,15},{4,8},{5,1},{6,10},{7,3},{8,12},{9,5},{1... | collective-permute-start | bytes 2359304 | tf_op jit(solution)/shard_map/ppermute | solution.py:34
  46.1 26.2 %collective-permute-start.12 = (f32[32,6144]{1,0:T(8,128)S(1)}, f32[32,6144]{1,0:T(8,128)S(1)}, u32[]{:S(2)}, u32[]{:S(2)}) collective-permute-start(f32[32,6144]{1,0:T(8,128)S(1)} %collective-permute-done.8), channel_id=1, source_target_pairs={{0,2},{1,3},{2,0},{3,1},{4,6},{5,7},{6,4},{7,5},{8,10},{9,11},{10,... | collective-permute-start | bytes 2359304 | tf_op jit(solution)/shard_map/ppermute | solution.py:34
  54.6 17.7 %collective-permute-start.11 = (f32[32,6144]{1,0:T(8,128)S(1)}, f32[32,6144]{1,0:T(8,128)S(1)}, u32[]{:S(2)}, u32[]{:S(2)}) collective-permute-start(f32[32,6144]{1,0:T(8,128)S(1)} %collective-permute-done.7), channel_id=1, source_target_pairs={{0,4},{1,13},{2,6},{3,15},{4,8},{5,1},{6,10},{7,3},{8,12},{9,5},{1... | collective-permute-start | bytes 2359304 | tf_op jit(solution)/shard_map/ppermute | solution.py:34
  57.7 22.2 %collective-permute-start.14 = (f32[32,6144]{1,0:T(8,128)S(1)}, f32[32,6144]{1,0:T(8,128)S(1)}, u32[]{:S(2)}, u32[]{:S(2)}) collective-permute-start(f32[32,6144]{1,0:T(8,128)S(1)} %collective-permute-done.13), channel_id=1, source_target_pairs={{0,4},{1,13},{2,6},{3,15},{4,8},{5,1},{6,10},{7,3},{8,12},{9,5},{1... | collective-permute-start | bytes 2359304 | tf_op jit(solution)/shard_map/ppermute | solution.py:34
  63.0 58.1 %collective-permute-start.6 = (f32[32,6144]{1,0:T(8,128)}, f32[32,6144]{1,0:T(8,128)}, u32[]{:S(2)}, u32[]{:S(2)}) collective-permute-start(f32[32,6144]{1,0:T(8,128)} %collective-permute-done.5), channel_id=1, source_target_pairs={{0,4},{1,13},{2,6},{3,15},{4,8},{5,1},{6,10},{7,3},{8,12},{9,5},{1... | collective-permute-start | bytes 2359304 | tf_op jit(solution)/shard_map/ppermute | solution.py:34
  66.3 2.7 %copy-start.1 = (f32[256,6144]{1,0:T(8,128)}, f32[256,6144]{1,0:T(8,128)S(1)}, u32[]{:S(2)}) copy-start(f32[256,6144]{1,0:T(8,128)S(1)} %constant_dynamic-update-slice_fusion.4) | copy-start | bytes 18874372
  68.9 10.9 %copy-start = (f32[6144,256]{1,0:T(8,128)}, f32[6144,256]{1,0:T(8,128)S(1)}, u32[]{:S(2)}) copy-start(f32[6144,256]{1,0:T(8,128)S(1)} %constant_dynamic-update-slice_fusion) | copy-start | bytes 18874372
  82.7 19.9 %all-to-all-start.1 = ((f32[16,8,256]{2,1,0:T(8,128)}), f32[16,8,256]{2,1,0:T(8,128)S(1)}, u32[]{:S(2)}, u32[]{:S(2)}) async-start(f32[16,8,256]{2,1,0:T(8,128)} %fusion.22), calls=%async_computation.1 | async-start | bytes 262144 | tf_op jit(solution)/shard_map/all_to_all | solution.py:63
  102.6 14.2 %all-to-all-start = ((f32[16,8,256]{2,1,0:T(8,128)}), f32[16,8,256]{2,1,0:T(8,128)S(1)}, u32[]{:S(2)}, u32[]{:S(2)}) async-start(f32[16,8,256]{2,1,0:T(8,128)} %fusion.25), calls=%async_computation | async-start | bytes 262144 | tf_op jit(solution)/shard_map/all_to_all | solution.py:63
  117.6 12.9 %all-to-all-start.2 = ((f32[16,2,8,256]{3,2,1,0:T(8,128)}), f32[16,2,8,256]{3,2,1,0:T(8,128)S(1)}, u32[]{:S(2)}, u32[]{:S(2)}) async-start(f32[16,2,8,256]{3,2,1,0:T(8,128)} %broadcast_in_dim.4), calls=%async_computation.2 | async-start | bytes 524288 | tf_op jit(solution)/shard_map/all_to_all | solution.py:66
  140.8 11.0 %copy-start.3 = (f32[6144,128]{1,0:T(8,128)S(1)}, f32[6144,128]{1,0:T(8,128)}, u32[]{:S(2)}) copy-start(f32[6144,128]{1,0:T(8,128)} %param.7) | copy-start | bytes 9437188
  140.9 7.9 %collective-permute-start.15 = (f32[2048,128]{1,0:T(8,128)S(1)}, f32[2048,128]{1,0:T(8,128)S(1)}, u32[]{:S(2)}, u32[]{:S(2)}) collective-permute-start(f32[2048,128]{1,0:T(8,128)S(1)} %slice.50), channel_id=1, source_target_pairs={{0,1},{1,0},{2,3},{3,2},{4,5},{5,4},{6,7},{7,6},{8,9},{9,8},{10,11... | collective-permute-start | bytes 3145736 | tf_op jit(solution)/shard_map/ppermute | solution.py:47
  146.6 3.7 %collective-permute-start.17 = (f32[2048,128]{1,0:T(8,128)S(1)}, f32[2048,128]{1,0:T(8,128)S(1)}, u32[]{:S(2)}, u32[]{:S(2)}) collective-permute-start(f32[2048,128]{1,0:T(8,128)S(1)} %slice.56), channel_id=1, source_target_pairs={{0,1},{1,0},{2,3},{3,2},{4,5},{5,4},{6,7},{7,6},{8,9},{9,8},{10,11... | collective-permute-start | bytes 3145736 | tf_op jit(solution)/shard_map/ppermute | solution.py:47
  146.8 5.0 %collective-permute-start.16 = (f32[2048,128]{1,0:T(8,128)S(1)}, f32[2048,128]{1,0:T(8,128)S(1)}, u32[]{:S(2)}, u32[]{:S(2)}) collective-permute-start(f32[2048,128]{1,0:T(8,128)S(1)} %slice.53), channel_id=1, source_target_pairs={{0,1},{1,0},{2,3},{3,2},{4,5},{5,4},{6,7},{7,6},{8,9},{9,8},{10,11... | collective-permute-start | bytes 3145736 | tf_op jit(solution)/shard_map/ppermute | solution.py:47

commit v3 on v2

--- a/solution.py
+++ b/solution.py
@@ -4,13 +4,13 @@
 from jax.sharding import PartitionSpec as P
 
 ROUTES = (
+    (0, "-", "+"),
     (0, "+", "-"),
-    (0, "-", "+"),
     (0, "y", "y"),
-    (1, "+", "-"),
+    (1, "-", "+"),
     (2, "y", "y"),
-    (3, "+", "-"),
-    (6, "+", "-"),
+    (3, "-", "+"),
+    (6, "-", "+"),
 )
 C_CHUNKS = 3
 

time: 155 us -> 154 us (level)
  starting transfers between devices: 50.5 us -> 41.9 us
  waiting for transfers between devices: 72.5 us -> 80.3 us
    ppermute x14, waiting for transfers between devices: 50.3 us -> 57.9 us  [gather_blocks(): held.append(lax.ppermute(held[source], 'pcol', pairs(moves)))]
    ppermute x14, starting transfers between devices: 21.4 us -> 16.8 us  [gather_blocks(): held.append(lax.ppermute(held[source], 'pcol', pairs(moves)))]
    ppermute x4, starting transfers between devices: 9.35 us -> 5.16 us  [swapped(): return lax.ppermute(x, 'pcol', [(at, at ^ 1) for at in range(16)])]
  transfers between devices with their start and end apart: 21 -> 21, of which waited for: 14 -> 17; matrix products, arithmetic and copies ran while one was open for 10% -> 10% of each run, Pallas kernels for 0% -> 0%
where the time goes in v3:
time: 154 us; the launch traced here: 153 us
  waiting for transfers between devices  80.3 us (52%)
  starting transfers between devices  41.9 us (27%)
  matrix products  18.4 us (12%)
  local copies, waits for them, and re-layouts  10.1 us (7%)
  other arithmetic  2.35 us (2%)
    ppermute x14, waiting for transfers between devices, gather_blocks(): held.append(lax.ppermute(held[source], 'pcol', pairs(moves)))  57.9 us
    dot_general x5, matrix products, product(): jnp.dot(a, b, precision=lax.Precision.HIGH, preferred_element_type=jnp.fl...  18.4 us
    ppermute x14, starting transfers between devices, gather_blocks(): held.append(lax.ppermute(held[source], 'pcol', pairs(moves)))  16.8 us
    all_to_all x2, starting transfers between devices, on_device(): tiles = lax.all_to_all(tiles, 'prow', 0, 0, tiled=True)  16.4 us
    all_to_all x2, waiting for transfers between devices, on_device(): tiles = lax.all_to_all(tiles, 'prow', 0, 0, tiled=True)  10.6 us
    all_to_all x1, waiting for transfers between devices, on_device(): inner = lax.all_to_all(copies, 'prow', 0, 0, tiled=True)  7.36 us
    dynamic_update_slice x8, local copies, waits for them, and re-layouts, placed_blocks(): out = lax.dynamic_update_slice(out, block, (i * k, 0))  6.24 us
    ppermute x4, starting transfers between devices, swapped(): return lax.ppermute(x, 'pcol', [(at, at ^ 1) for at in range(16)])  5.16 us
  transfers between devices with their start and end apart: 21, of which 17 were waited for; matrix products, arithmetic and copies ran while one was open for 10% of the time, Pallas kernels for 0%

profile of v3, /device:TPU:1, one launch (start us, length us, event | category | flops | bytes accessed | tf_op | source)
XLA Modules:
  0.0 153.2 jit_solution(12297494399950022262)
XLA Ops:
  0.0 2.0 %collective-permute-start = (f32[32,6144]{1,0:T(8,128)}, f32[32,6144]{1,0:T(8,128)S(1)}, u32[]{:S(2)}, u32[]{:S(2)}) collective-permute-start(f32[32,6144]{1,0:T(8,128)} %param.5), channel_id=1, source_target_pairs={{0,12},{1,5},{2,14},{3,7},{4,0},{5,9},{6,2},{7,11},{8,4},{9,13},{1... | collective-permute-start | bytes 2359304 | tf_op jit(solution)/shard_map/ppermute | solution.py:34
  3.3 1.5 collective-permute-start.9
  6.6 1.8 %dynamic_update_slice.24 = f32[256,6144]{1,0:T(8,128)S(1)} pad(f32[32,6144]{1,0:T(8,128)} %param.5, f32[]{:T(128)} %constant.9.clone.1), padding=0_224x0_0 | pad | bytes 7077892 | tf_op jit(solution)/shard_map/dynamic_update_slice | solution.py:42
  8.7 8.8 %collective-permute-done = f32[32,6144]{1,0:T(8,128)S(1)} collective-permute-done((f32[32,6144]{1,0:T(8,128)}, f32[32,6144]{1,0:T(8,128)S(1)}, u32[]{:S(2)}, u32[]{:S(2)}) %collective-permute-start) | collective-permute-done | bytes 786464 | tf_op jit(solution)/shard_map/ppermute | solution.py:34
  17.5 1.7 %collective-permute-start.2 = (f32[32,6144]{1,0:T(8,128)S(1)}, f32[32,6144]{1,0:T(8,128)S(1)}, u32[]{:S(2)}, u32[]{:S(2)}) collective-permute-start(f32[32,6144]{1,0:T(8,128)S(1)} %copy-done.4), channel_id=1, source_target_pairs={{0,2},{1,3},{2,0},{3,1},{4,6},{5,7},{6,4},{7,5},{8,10},{9,11},{10,... | collective-permute-start | bytes 2359304 | tf_op jit(solution)/shard_map/ppermute | solution.py:34
  20.2 2.8 %collective-permute-start.3 = (f32[32,6144]{1,0:T(8,128)S(1)}, f32[32,6144]{1,0:T(8,128)S(1)}, u32[]{:S(2)}, u32[]{:S(2)}) collective-permute-start(f32[32,6144]{1,0:T(8,128)S(1)} %collective-permute-done), channel_id=1, source_target_pairs={{0,12},{1,5},{2,14},{3,7},{4,0},{5,9},{6,2},{7,11},{8,4},{9,13},{1... | collective-permute-start | bytes 2359304 | tf_op jit(solution)/shard_map/ppermute | solution.py:34
  23.9 9.3 %collective-permute-done.8 = f32[32,6144]{1,0:T(8,128)S(1)} collective-permute-done((f32[32,6144]{1,0:T(8,128)}, f32[32,6144]{1,0:T(8,128)S(1)}, u32[]{:S(2)}, u32[]{:S(2)}) %collective-permute-start.8) | collective-permute-done | bytes 786464 | tf_op jit(solution)/shard_map/ppermute | solution.py:34
  34.1 2.7 %collective-permute-done.2 = f32[32,6144]{1,0:T(8,128)S(1)} collective-permute-done((f32[32,6144]{1,0:T(8,128)S(1)}, f32[32,6144]{1,0:T(8,128)S(1)}, u32[]{:S(2)}, u32[]{:S(2)}) %collective-permute-start.2) | collective-permute-done | bytes 786464 | tf_op jit(solution)/shard_map/ppermute | solution.py:34
  38.8 7.8 %collective-permute-done.7 = f32[32,6144]{1,0:T(8,128)S(1)} collective-permute-done((f32[32,6144]{1,0:T(8,128)S(1)}, f32[32,6144]{1,0:T(8,128)S(1)}, u32[]{:S(2)}, u32[]{:S(2)}) %collective-permute-start.7) | collective-permute-done | bytes 786464 | tf_op jit(solution)/shard_map/ppermute | solution.py:34
  46.6 1.5 collective-permute-start.12
  48.1 6.9 %collective-permute-done.13 = f32[32,6144]{1,0:T(8,128)S(1)} collective-permute-done((f32[32,6144]{1,0:T(8,128)S(1)}, f32[32,6144]{1,0:T(8,128)S(1)}, u32[]{:S(2)}, u32[]{:S(2)}) %collective-permute-start.13) | collective-permute-done | bytes 786464 | tf_op jit(solution)/shard_map/ppermute | solution.py:34
  56.7 6.8 %collective-permute-done.5 = f32[32,6144]{1,0:T(8,128)} collective-permute-done((f32[32,6144]{1,0:T(8,128)S(1)}, f32[32,6144]{1,0:T(8,128)}, u32[]{:S(2)}, u32[]{:S(2)}) %collective-permute-start.5) | collective-permute-done | bytes 786464 | tf_op jit(solution)/shard_map/ppermute | solution.py:34
  64.4 2.4 %copy-done.1 = f32[256,6144]{1,0:T(8,128)} copy-done((f32[256,6144]{1,0:T(8,128)}, f32[256,6144]{1,0:T(8,128)S(1)}, u32[]{:S(2)}) %copy-start.1) | copy-done | bytes 6291480
  66.8 3.8 %collective-permute-done.12 = f32[32,6144]{1,0:T(8,128)S(1)} collective-permute-done((f32[32,6144]{1,0:T(8,128)S(1)}, f32[32,6144]{1,0:T(8,128)S(1)}, u32[]{:S(2)}, u32[]{:S(2)}) %collective-permute-start.12) | collective-permute-done | bytes 786464 | tf_op jit(solution)/shard_map/ppermute | solution.py:34
  71.9 8.4 %collective-permute-done.14 = f32[32,6144]{1,0:T(8,128)S(1)} collective-permute-done((f32[32,6144]{1,0:T(8,128)S(1)}, f32[32,6144]{1,0:T(8,128)S(1)}, u32[]{:S(2)}, u32[]{:S(2)}) %collective-permute-start.14) | collective-permute-done | bytes 786464 | tf_op jit(solution)/shard_map/ppermute | solution.py:34
  80.3 2.9 %fusion.22 = f32[16,8,256]{2,1,0:T(8,128)} fusion(f32[6144,256]{1,0:T(8,128)S(1)} %constant_dynamic-update-slice_fusion, f32[32,6144]{1,0:T(8,128)S(1)} %collective-permute-done.14, f32[32,6144]{1,0:T(8,128)S(1)} %collective-permute-done.13, f32[32,6144]{1,0:T(8,128)S(1)} %collective-permute-done.12, f32[32,6144]{1,0:T(8,128)S(1)} %collective-permute-done.11), kind=kOutput, calls=%fused_computation.23 | convolution fusion | flops 1210318848 | bytes 9568256 | tf_op jit(solution)/shard_map/dot_general | solution.py:51
  83.2 11.1 %all-to-all-start.1 = ((f32[16,8,256]{2,1,0:T(8,128)}), f32[16,8,256]{2,1,0:T(8,128)S(1)}, u32[]{:S(2)}, u32[]{:S(2)}) async-start(f32[16,8,256]{2,1,0:T(8,128)} %fusion.22), calls=%async_computation.1 | async-start | bytes 262144 | tf_op jit(solution)/shard_map/all_to_all | solution.py:63
  94.3 5.2 %fusion.25 = f32[16,8,256]{2,1,0:T(8,128)} fusion(f32[6144,256]{1,0:T(8,128)} %copy-done, f32[32,6144]{1,0:T(8,128)S(1)} %collective-permute-done.9, f32[32,6144]{1,0:T(8,128)S(1)} %collective-permute-done.8, f32[32,6144]{1,0:T(8,128)S(1)} %collective-permute-done.7, f32[32,6144]{1,0:T(8,128)S(1)} %bitcast.21), kind=kOutput, calls=%fused_computation.24 | convolution fusion | flops 1210318848 | bytes 9568256 | tf_op jit(solution)/shard_map/dot_general | solution.py:51
  99.5 3.8 %all-to-all-done.1 = f32[16,8,256]{2,1,0:T(8,128)S(1)} async-done(((f32[16,8,256]{2,1,0:T(8,128)}), f32[16,8,256]{2,1,0:T(8,128)S(1)}, u32[]{:S(2)}, u32[]{:S(2)}) %all-to-all-start.1) | async-done | bytes 131104 | tf_op jit(solution)/shard_map/all_to_all | solution.py:63
  103.2 5.3 %all-to-all-start = ((f32[16,8,256]{2,1,0:T(8,128)}), f32[16,8,256]{2,1,0:T(8,128)S(1)}, u32[]{:S(2)}, u32[]{:S(2)}) async-start(f32[16,8,256]{2,1,0:T(8,128)} %fusion.25), calls=%async_computation | async-start | bytes 262144 | tf_op jit(solution)/shard_map/all_to_all | solution.py:63
  108.5 2.1 %constant_dynamic-update-slice_fusion.3 = f32[256,6144]{1,0:T(8,128)} fusion(f32[256,6144]{1,0:T(8,128)} %copy-done.1, f32[32,6144]{1,0:T(8,128)} %collective-permute-done.5), kind=kLoop, calls=%fused_computation.35 | loop fusion | bytes 1572864 | tf_op jit(solution)/shard_map/dynamic_update_slice | solution.py:42
  110.6 6.8 %all-to-all-done = f32[16,8,256]{2,1,0:T(8,128)S(1)} async-done(((f32[16,8,256]{2,1,0:T(8,128)}), f32[16,8,256]{2,1,0:T(8,128)S(1)}, u32[]{:S(2)}, u32[]{:S(2)}) %all-to-all-start) | async-done | bytes 131104 | tf_op jit(solution)/shard_map/all_to_all | solution.py:63
  118.2 3.5 %all-to-all-start.2 = ((f32[16,2,8,256]{3,2,1,0:T(8,128)}), f32[16,2,8,256]{3,2,1,0:T(8,128)S(1)}, u32[]{:S(2)}, u32[]{:S(2)}) async-start(f32[16,2,8,256]{3,2,1,0:T(8,128)} %broadcast_in_dim.4), calls=%async_computation.2 | async-start | bytes 524288 | tf_op jit(solution)/shard_map/all_to_all | solution.py:66
  121.8 2.1 %constant_dynamic-update-slice_fusion.2 = f32[256,6144]{1,0:T(8,128)} fusion(f32[256,6144]{1,0:T(8,128)} %constant_dynamic-update-slice_fusion.3, f32[32,6144]{1,0:T(8,128)} %collective-permute-done.6), kind=kLoop, calls=%fused_computation.34 | loop fusion | bytes 1572864 | tf_op jit(solution)/shard_map/dynamic_update_slice | solution.py:42
  123.9 7.4 %all-to-all-done.2 = f32[16,2,8,256]{3,2,1,0:T(8,128)S(1)} async-done(((f32[16,2,8,256]{3,2,1,0:T(8,128)}), f32[16,2,8,256]{3,2,1,0:T(8,128)S(1)}, u32[]{:S(2)}, u32[]{:S(2)}) %all-to-all-start.2) | async-done | bytes 262176 | tf_op jit(solution)/shard_map/all_to_all | solution.py:66
  131.2 3.4 %fusion.20 = f32[2048,256]{1,0:T(8,128)S(1)} fusion(f32[256,256]{1,0:T(8,128)S(1)} %bitcast.15, f32[256,6144]{1,0:T(8,128)} %constant_dynamic-update-slice_fusion.2), kind=kOutput, calls=%fused_computation.21 | convolution fusion | flops 805306368 | bytes 4456448 | tf_op jit(solution)/shard_map/dot_general | solution.py:51
  134.7 3.4 %fusion.16 = f32[2048,256]{1,0:T(8,128)S(1)} fusion(f32[256,256]{1,0:T(8,128)S(1)} %bitcast.16, f32[256,6144]{1,0:T(8,128)} %constant_dynamic-update-slice_fusion.2), kind=kOutput, calls=%fused_computation.17 | convolution fusion | flops 805306368 | bytes 4456448 | tf_op jit(solution)/shard_map/dot_general | solution.py:51
  138.1 3.4 %fusion.18 = f32[2048,256]{1,0:T(8,128)S(1)} fusion(f32[256,256]{1,0:T(8,128)S(1)} %bitcast.17, f32[256,6144]{1,0:T(8,128)} %constant_dynamic-update-slice_fusion.2), kind=kOutput, calls=%fused_computation.19 | convolution fusion | flops 805306368 | bytes 4456448 | tf_op jit(solution)/shard_map/dot_general | solution.py:51
  141.7 3.9 %collective-permute-start.15 = (f32[2048,128]{1,0:T(8,128)S(1)}, f32[2048,128]{1,0:T(8,128)S(1)}, u32[]{:S(2)}, u32[]{:S(2)}) collective-permute-start(f32[2048,128]{1,0:T(8,128)S(1)} %slice.50), channel_id=1, source_target_pairs={{0,1},{1,0},{2,3},{3,2},{4,5},{5,4},{6,7},{7,6},{8,9},{9,8},{10,11... | collective-permute-start | bytes 3145736 | tf_op jit(solution)/shard_map/ppermute | solution.py:47
  147.9 1.5 collective-permute-done.17
  149.4 1.5 collective-permute-done.16
  151.4 1.9 %pad_maximum_fusion = f32[6144,128]{1,0:T(8,128)} fusion(f32[2048,128]{1,0:T(8,128)S(1)} %get-tuple-element.6, f32[2048,128]{1,0:T(8,128)S(1)} %get-tuple-element.7, f32[2048,128]{1,0:T(8,128)S(1)} %get-tuple-element.5), kind=kLoop, calls=%fused_computation.16 | loop fusion | flops 1572864 | bytes 6291456 | tf_op jit(solution)/shard_map/concatenate | solution.py:75
  (47 shorter events, 15.6 us)
Async XLA Ops:
  0.0 17.5 %collective-permute-start = (f32[32,6144]{1,0:T(8,128)}, f32[32,6144]{1,0:T(8,128)S(1)}, u32[]{:S(2)}, u32[]{:S(2)}) collective-permute-start(f32[32,6144]{1,0:T(8,128)} %param.5), channel_id=1, source_target_pairs={{0,12},{1,5},{2,14},{3,7},{4,0},{5,9},{6,2},{7,11},{8,4},{9,13},{1... | collective-permute-start | bytes 2359304 | tf_op jit(solution)/shard_map/ppermute | solution.py:34
  2.0 18.1 %collective-permute-start.1 = (f32[32,6144]{1,0:T(8,128)}, f32[32,6144]{1,0:T(8,128)S(1)}, u32[]{:S(2)}, u32[]{:S(2)}) collective-permute-start(f32[32,6144]{1,0:T(8,128)} %param.5), channel_id=1, source_target_pairs={{0,4},{1,13},{2,6},{3,15},{4,8},{5,1},{6,10},{7,3},{8,12},{9,5},{1... | collective-permute-start | bytes 2359304 | tf_op jit(solution)/shard_map/ppermute | solution.py:34
  3.3 5.1 %copy-start.2 = (f32[6144,128]{1,0:T(8,128)S(1)}, f32[6144,128]{1,0:T(8,128)}, u32[]{:S(2)}) copy-start(f32[6144,128]{1,0:T(8,128)} %param.6) | copy-start | bytes 9437188
  3.3 19.8 %collective-permute-start.9 = (f32[32,6144]{1,0:T(8,128)}, f32[32,6144]{1,0:T(8,128)S(1)}, u32[]{:S(2)}, u32[]{:S(2)}) collective-permute-start(f32[32,6144]{1,0:T(8,128)} %bitcast.18), channel_id=1, source_target_pairs={{0,2},{1,3},{2,0},{3,1},{4,6},{5,7},{6,4},{7,5},{8,10},{9,11},{10,... | collective-permute-start | bytes 2359304 | tf_op jit(solution)/shard_map/ppermute | solution.py:34
  4.8 28.4 %collective-permute-start.8 = (f32[32,6144]{1,0:T(8,128)}, f32[32,6144]{1,0:T(8,128)S(1)}, u32[]{:S(2)}, u32[]{:S(2)}) collective-permute-start(f32[32,6144]{1,0:T(8,128)} %bitcast.19), channel_id=1, source_target_pairs={{0,4},{1,13},{2,6},{3,15},{4,8},{5,1},{6,10},{7,3},{8,12},{9,5},{1... | collective-permute-start | bytes 2359304 | tf_op jit(solution)/shard_map/ppermute | solution.py:34
  6.1 58.0 %collective-permute-start.10 = (f32[6144,128]{1,0:T(8,128)}, f32[6144,128]{1,0:T(8,128)S(1)}, u32[]{:S(2)}, u32[]{:S(2)}) collective-permute-start(f32[6144,128]{1,0:T(8,128)} %param.6), channel_id=1, source_target_pairs={{0,1},{1,0},{2,3},{3,2},{4,5},{5,4},{6,7},{7,6},{8,9},{9,8},{10,11... | collective-permute-start | bytes 9437192 | tf_op jit(solution)/shard_map/ppermute | solution.py:47
  8.4 9.1 %copy-start.4 = (f32[32,6144]{1,0:T(8,128)S(1)}, f32[32,6144]{1,0:T(8,128)}, u32[]{:S(2)}) copy-start(f32[32,6144]{1,0:T(8,128)} %param.5) | copy-start | bytes 2359300
  8.4 14.6 %copy-start.5 = (f32[6144,32]{0,1:T(8,128)S(1)}, f32[6144,32]{0,1:T(8,128)}, u32[]{:S(2)}) copy-start(f32[6144,32]{0,1:T(8,128)} %param.4) | copy-start | bytes 2359300
  17.5 19.3 %collective-permute-start.2 = (f32[32,6144]{1,0:T(8,128)S(1)}, f32[32,6144]{1,0:T(8,128)S(1)}, u32[]{:S(2)}, u32[]{:S(2)}) collective-permute-start(f32[32,6144]{1,0:T(8,128)S(1)} %copy-done.4), channel_id=1, source_target_pairs={{0,2},{1,3},{2,0},{3,1},{4,6},{5,7},{6,4},{7,5},{8,10},{9,11},{10,... | collective-permute-start | bytes 2359304 | tf_op jit(solution)/shard_map/ppermute | solution.py:34
  20.2 18.0 %collective-permute-start.3 = (f32[32,6144]{1,0:T(8,128)S(1)}, f32[32,6144]{1,0:T(8,128)S(1)}, u32[]{:S(2)}, u32[]{:S(2)}) collective-permute-start(f32[32,6144]{1,0:T(8,128)S(1)} %collective-permute-done), channel_id=1, source_target_pairs={{0,12},{1,5},{2,14},{3,7},{4,0},{5,9},{6,2},{7,11},{8,4},{9,13},{1... | collective-permute-start | bytes 2359304 | tf_op jit(solution)/shard_map/ppermute | solution.py:34
  23.1 23.5 %collective-permute-start.7 = (f32[32,6144]{1,0:T(8,128)S(1)}, f32[32,6144]{1,0:T(8,128)S(1)}, u32[]{:S(2)}, u32[]{:S(2)}) collective-permute-start(f32[32,6144]{1,0:T(8,128)S(1)} %bitcast.20), channel_id=1, source_target_pairs={{0,12},{1,5},{2,14},{3,7},{4,0},{5,9},{6,2},{7,11},{8,4},{9,13},{1... | collective-permute-start | bytes 2359304 | tf_op jit(solution)/shard_map/ppermute | solution.py:34
  33.2 22.3 %collective-permute-start.4 = (f32[32,6144]{1,0:T(8,128)S(1)}, f32[32,6144]{1,0:T(8,128)S(1)}, u32[]{:S(2)}, u32[]{:S(2)}) collective-permute-start(f32[32,6144]{1,0:T(8,128)S(1)} %collective-permute-done.1), channel_id=1, source_target_pairs={{0,2},{1,3},{2,0},{3,1},{4,6},{5,7},{6,4},{7,5},{8,10},{9,11},{10,... | collective-permute-start | bytes 2359304 | tf_op jit(solution)/shard_map/ppermute | solution.py:34
  36.8 18.2 %collective-permute-start.13 = (f32[32,6144]{1,0:T(8,128)S(1)}, f32[32,6144]{1,0:T(8,128)S(1)}, u32[]{:S(2)}, u32[]{:S(2)}) collective-permute-start(f32[32,6144]{1,0:T(8,128)S(1)} %collective-permute-done.9), channel_id=1, source_target_pairs={{0,12},{1,5},{2,14},{3,7},{4,0},{5,9},{6,2},{7,11},{8,4},{9,13},{1... | collective-permute-start | bytes 2359304 | tf_op jit(solution)/shard_map/ppermute | solution.py:34
  38.2 25.4 %collective-permute-start.5 = (f32[32,6144]{1,0:T(8,128)S(1)}, f32[32,6144]{1,0:T(8,128)}, u32[]{:S(2)}, u32[]{:S(2)}) collective-permute-start(f32[32,6144]{1,0:T(8,128)S(1)} %collective-permute-done.2), channel_id=1, source_target_pairs={{0,12},{1,5},{2,14},{3,7},{4,0},{5,9},{6,2},{7,11},{8,4},{9,13},{1... | collective-permute-start | bytes 2359304 | tf_op jit(solution)/shard_map/ppermute | solution.py:34
  46.6 23.9 %collective-permute-start.12 = (f32[32,6144]{1,0:T(8,128)S(1)}, f32[32,6144]{1,0:T(8,128)S(1)}, u32[]{:S(2)}, u32[]{:S(2)}) collective-permute-start(f32[32,6144]{1,0:T(8,128)S(1)} %collective-permute-done.8), channel_id=1, source_target_pairs={{0,2},{1,3},{2,0},{3,1},{4,6},{5,7},{6,4},{7,5},{8,10},{9,11},{10,... | collective-permute-start | bytes 2359304 | tf_op jit(solution)/shard_map/ppermute | solution.py:34
  55.0 16.9 %collective-permute-start.11 = (f32[32,6144]{1,0:T(8,128)S(1)}, f32[32,6144]{1,0:T(8,128)S(1)}, u32[]{:S(2)}, u32[]{:S(2)}) collective-permute-start(f32[32,6144]{1,0:T(8,128)S(1)} %collective-permute-done.7), channel_id=1, source_target_pairs={{0,12},{1,5},{2,14},{3,7},{4,0},{5,9},{6,2},{7,11},{8,4},{9,13},{1... | collective-permute-start | bytes 2359304 | tf_op jit(solution)/shard_map/ppermute | solution.py:34
  55.5 24.8 %collective-permute-start.14 = (f32[32,6144]{1,0:T(8,128)S(1)}, f32[32,6144]{1,0:T(8,128)S(1)}, u32[]{:S(2)}, u32[]{:S(2)}) collective-permute-start(f32[32,6144]{1,0:T(8,128)S(1)} %collective-permute-done.13), channel_id=1, source_target_pairs={{0,12},{1,5},{2,14},{3,7},{4,0},{5,9},{6,2},{7,11},{8,4},{9,13},{1... | collective-permute-start | bytes 2359304 | tf_op jit(solution)/shard_map/ppermute | solution.py:34
  63.5 58.2 %collective-permute-start.6 = (f32[32,6144]{1,0:T(8,128)}, f32[32,6144]{1,0:T(8,128)}, u32[]{:S(2)}, u32[]{:S(2)}) collective-permute-start(f32[32,6144]{1,0:T(8,128)} %collective-permute-done.5), channel_id=1, source_target_pairs={{0,12},{1,5},{2,14},{3,7},{4,0},{5,9},{6,2},{7,11},{8,4},{9,13},{1... | collective-permute-start | bytes 2359304 | tf_op jit(solution)/shard_map/ppermute | solution.py:34
  64.1 2.7 %copy-start.1 = (f32[256,6144]{1,0:T(8,128)}, f32[256,6144]{1,0:T(8,128)S(1)}, u32[]{:S(2)}) copy-start(f32[256,6144]{1,0:T(8,128)S(1)} %constant_dynamic-update-slice_fusion.4) | copy-start | bytes 18874372
  66.8 13.5 %copy-start = (f32[6144,256]{1,0:T(8,128)}, f32[6144,256]{1,0:T(8,128)S(1)}, u32[]{:S(2)}) copy-start(f32[6144,256]{1,0:T(8,128)S(1)} %constant_dynamic-update-slice_fusion) | copy-start | bytes 18874372
  83.2 20.1 %all-to-all-start.1 = ((f32[16,8,256]{2,1,0:T(8,128)}), f32[16,8,256]{2,1,0:T(8,128)S(1)}, u32[]{:S(2)}, u32[]{:S(2)}) async-start(f32[16,8,256]{2,1,0:T(8,128)} %fusion.22), calls=%async_computation.1 | async-start | bytes 262144 | tf_op jit(solution)/shard_map/all_to_all | solution.py:63
  103.2 14.2 %all-to-all-start = ((f32[16,8,256]{2,1,0:T(8,128)}), f32[16,8,256]{2,1,0:T(8,128)S(1)}, u32[]{:S(2)}, u32[]{:S(2)}) async-start(f32[16,8,256]{2,1,0:T(8,128)} %fusion.25), calls=%async_computation | async-start | bytes 262144 | tf_op jit(solution)/shard_map/all_to_all | solution.py:63
  118.2 13.0 %all-to-all-start.2 = ((f32[16,2,8,256]{3,2,1,0:T(8,128)}), f32[16,2,8,256]{3,2,1,0:T(8,128)S(1)}, u32[]{:S(2)}, u32[]{:S(2)}) async-start(f32[16,2,8,256]{3,2,1,0:T(8,128)} %broadcast_in_dim.4), calls=%async_computation.2 | async-start | bytes 524288 | tf_op jit(solution)/shard_map/all_to_all | solution.py:66
  141.6 9.3 %copy-start.3 = (f32[6144,128]{1,0:T(8,128)S(1)}, f32[6144,128]{1,0:T(8,128)}, u32[]{:S(2)}) copy-start(f32[6144,128]{1,0:T(8,128)} %param.7) | copy-start | bytes 9437188
  141.7 6.2 %collective-permute-start.15 = (f32[2048,128]{1,0:T(8,128)S(1)}, f32[2048,128]{1,0:T(8,128)S(1)}, u32[]{:S(2)}, u32[]{:S(2)}) collective-permute-start(f32[2048,128]{1,0:T(8,128)S(1)} %slice.50), channel_id=1, source_target_pairs={{0,1},{1,0},{2,3},{3,2},{4,5},{5,4},{6,7},{7,6},{8,9},{9,8},{10,11... | collective-permute-start | bytes 3145736 | tf_op jit(solution)/shard_map/ppermute | solution.py:47
  145.7 3.7 %collective-permute-start.17 = (f32[2048,128]{1,0:T(8,128)S(1)}, f32[2048,128]{1,0:T(8,128)S(1)}, u32[]{:S(2)}, u32[]{:S(2)}) collective-permute-start(f32[2048,128]{1,0:T(8,128)S(1)} %slice.56), channel_id=1, source_target_pairs={{0,1},{1,0},{2,3},{3,2},{4,5},{5,4},{6,7},{7,6},{8,9},{9,8},{10,11... | collective-permute-start | bytes 3145736 | tf_op jit(solution)/shard_map/ppermute | solution.py:47
  145.9 5.0 %collective-permute-start.16 = (f32[2048,128]{1,0:T(8,128)S(1)}, f32[2048,128]{1,0:T(8,128)S(1)}, u32[]{:S(2)}, u32[]{:S(2)}) collective-permute-start(f32[2048,128]{1,0:T(8,128)S(1)} %slice.53), channel_id=1, source_target_pairs={{0,1},{1,0},{2,3},{3,2},{4,5},{5,4},{6,7},{7,6},{8,9},{9,8},{10,11... | collective-permute-start | bytes 3145736 | tf_op jit(solution)/shard_map/ppermute | solution.py:47
